TPU v7x, 32 devices: a whole 2x2x4 slice. The times are simulated.
32 devices in a mesh: span: 2 (over y), height: 4 (over x, core), depth: 4 (over z).
Axes of the slice: x: 2, y: 2, z: 4, core: 2. Of those that a mesh axis runs over, the one named last changes fastest.
Arguments:
- load: float32 [8, 32, 64, 512], P(None, 'span', 'height', 'depth'), may hold values from -6 to 6
- phase: float32 [32, 64, 512], P('span', 'height', 'depth'), may hold values from 0.1 to 1
- void: int32 [4, 8, 64], P('span', 'height', 'depth'), may hold values from 0 to 1, as said below
- owner: int32 [4, 8, 64], P('span', 'height', 'depth'), may hold values from 0 to 1, as said below
- precond: bfloat16 [512, 512, 512], P(('span', 'height', 'depth')), may hold values from -1 to 2, as said below
Outputs:
- displacement: float32 [8, 32, 64, 512], P(None, 'span', 'height', 'depth')
- sensitivity: float32 [32, 64, 512], P('span', 'height', 'depth')
- phase_next: float32 [32, 64, 512], P('span', 'height', 'depth')
Inputs may be any that keep to these rules, and one draw needn't show every extreme that they name: `void`: each device's block of 16 x 16 x 128 cells holds at most 16 solid bricks; some device holds exactly 16. `owner`: among the solid bricks of one device at most 8 name any one value; on some device every value is named by exactly 8 solid bricks. Values of void bricks carry no meaning. `precond`: every block is symmetric with a positive diagonal that dominates each row.
All inputs are finite; a program needn't handle non-finite values.
Results may differ from a plain program's by a relative error of at most 0.0021.
Values may be sent and summed in bfloat16 or wider, within the bound.
No kernel may reach another device: no remote copies, remote signals or barrier semaphores. Data moves between devices by JAX's collectives and lax.ppermute only.
A program may use at most 128 MiB of HBM per device.

v0:
```python
import jax
import jax.numpy as jnp
from jax import lax
from jax.experimental import pallas as pl
from jax.experimental.pallas import tpu as pltpu
from jax.sharding import PartitionSpec as P


BE = 8
AXES = ("span", "height", "depth")

void_stiffness = 0.001
spring_rate = 0.05
time_step = 0.5
interface_weight = 0.5
epsilon_peak = 1e-06
inverse = 1.0 / (1.0 / time_step + 6.0 * interface_weight)

F32 = jnp.float32
BF16 = jnp.bfloat16
VM = pl.BlockSpec(memory_space=pltpu.VMEM)
SM = pl.BlockSpec(memory_space=pltpu.SMEM)


HB = pl.BlockSpec(memory_space=pltpu.HBM)


def call(kernel, ins, outs, scratch=(), flops=0, aliases=None):
    arrays = [
        pltpu.with_memory_space_constraint(
            array, pltpu.HBM if spec is HB else pltpu.SMEM if spec is SM else pltpu.VMEM
        )
        for array, spec in ins
    ]
    return pl.pallas_call(
        kernel,
        in_specs=[spec for _, spec in ins],
        out_specs=[spec for _, _, spec in outs],
        out_shape=[
            jax.ShapeDtypeStruct(shape, dtype)
            if spec is HB
            else (pltpu.SMEM if spec is SM else pltpu.VMEM)(shape, dtype)
            for shape, dtype, spec in outs
        ],
        scratch_shapes=list(scratch),
        input_output_aliases=aliases or {},
        cost_estimate=pl.CostEstimate(flops=flops, bytes_accessed=1 << 20, transcendentals=0),
        compiler_params=pltpu.CompilerParams(vmem_limit_bytes=12 << 20),
    )(*arrays)


def slots_fit(bricks, cells):
    return all(n * BE == size for n, size in zip(bricks, cells))


def local(load, phase, void, owner, precond):
    loads, X, Y, Z = load.shape
    bricks_x, bricks_y, bricks_z = void.shape
    bricks = bricks_x * bricks_y * bricks_z
    T = Y // BE
    tiles = X * T
    cells = BE**3
    lanes = Z
    assert lanes == 128 and BE == 8 and loads == 8 and slots_fit(void.shape, phase.shape)
    sizes = [lax.axis_size(axis) for axis in AXES]
    assert all(size % 2 == 0 for size in sizes)
    spans = sizes[0]
    devices = sizes[0] * sizes[1] * sizes[2]
    slots = precond.shape[0]
    cap = slots // spans
    bits = 32 // spans
    assert cap < (1 << min(bits, 8)) and bits >= 2
    remote = (spans - 1) * cap

    has_b = [size > 2 for size in sizes]
    faces = [(d, b) for d in range(3) for b in range(2) if b == 0 or has_b[d]]
    load_f = load.reshape(loads, X * Y, Z)
    phase_f = phase.reshape(X * Y, Z)

    def iotas():
        return (
            lax.broadcasted_iota(jnp.int32, (8, lanes), 0),
            lax.broadcasted_iota(jnp.int32, (8, lanes), 1),
        )

    def row(x, t):
        start = x * Y + t * 8
        return pl.ds(start if isinstance(start, int) else pl.multiple_of(start, 8), 8)

    def brick_at(n):
        m = jnp.maximum(n, 0)
        return m // (bricks_y * bricks_z), (m // bricks_z) % bricks_y, m % bricks_z

    def spread_of(rows, columns, row_part, column_part):
        r = lax.broadcasted_iota(jnp.int32, (rows, columns), 0)
        c = lax.broadcasted_iota(jnp.int32, (rows, columns), 1)
        same = jnp.logical_and(row_part(r) == column_part(c), (r & 7) == (c & 7))
        return jnp.where(same, 1.0, 0.0).astype(BF16)

    def halves(value):
        high = value.astype(BF16).astype(F32)
        return high, value - high

    def in_groups(count, one, group=4):
        while count % group:
            group //= 2

        def several(i, carry):
            for j in range(group):
                one(i * group + j)
            return carry

        lax.fori_loop(0, count // group, several, 0)

    def gather_bricks(source, table, base, count, out, group=4):
        sub, lane = iotas()
        keep = ((lane >> 3) & 7) == sub
        fold = spread_of(2 * lanes, lanes, lambda r: r >> 7, lambda c: c >> 6)
        pick = jnp.where(
            lax.broadcasted_iota(jnp.int32, (loads, loads * 8), 1) >> 3
            == lax.broadcasted_iota(jnp.int32, (loads, loads * 8), 0),
            1.0,
            0.0,
        ).astype(BF16)

        def one(r):
            n = table[base + r]
            bx, by, bz = brick_at(n)
            inside = (lane >> 3) == jnp.where(n >= 0, bz, -1)
            rows = []
            for q in range(4):
                for l in range(loads):
                    pair = [
                        jnp.where(inside, source[l, row(bx * 8 + 2 * q + h, by), :], 0.0)
                        for h in range(2)
                    ]
                    rows.append(jnp.concatenate(pair, axis=1))
            stacked = jnp.concatenate(rows, axis=0).astype(BF16)
            folded = jnp.dot(stacked, fold, preferred_element_type=F32)
            columns = []
            for q in range(4):
                columns.append(
                    jnp.concatenate(
                        [
                            jnp.where(
                                keep,
                                folded[(q * loads + l) * 8 : (q * loads + l + 1) * 8],
                                0.0,
                            )
                            for l in range(loads)
                        ],
                        axis=0,
                    )
                )
            cells_of = jnp.concatenate(columns, axis=1).astype(BF16)
            out[r] = jnp.dot(pick, cells_of, preferred_element_type=F32).astype(BF16)

        in_groups(count, one, group)

    def scatter_bricks(field, table, base, count, images, split):
        sub, lane = iotas()
        keep = ((lane >> 3) & 7) == sub
        unfold = spread_of(
            2 * lanes, 2 * lanes, lambda r: (r >> 6) & 1, lambda c: c >> 7
        )

        def one(r):
            n = table[base + r]
            bx, by, bz = brick_at(n)
            inside = (lane >> 3) == jnp.where(n >= 0, bz, -1)
            high, low = halves(images[r].astype(F32))
            split[r, 0] = high
            split[r, 1] = low
            rows = []
            for q in range(4):
                for l in range(loads):
                    pair = [
                        jnp.where(
                            keep,
                            jnp.broadcast_to(
                                split[r, part, pl.ds(l, 1), pl.ds(q * lanes, lanes)],
                                (8, lanes),
                            ),
                            0.0,
                        )
                        for part in range(2)
                    ]
                    rows.append(jnp.concatenate(pair, axis=1))
            stacked = jnp.concatenate(rows, axis=0).astype(BF16)
            spread = jnp.dot(stacked, unfold, preferred_element_type=F32)
            for q in range(4):
                for l in range(loads):
                    for h in range(2):
                        at = row(bx * 8 + 2 * q + h, by)
                        tile = spread[
                            (q * loads + l) * 8 : (q * loads + l + 1) * 8,
                            h * lanes : (h + 1) * lanes,
                        ]
                        field[l, at, :] = jnp.where(inside, tile, field[l, at, :])

        in_groups(count, one)

    def face_position(coords_ref, d, b, extent):
        high = (coords_ref[d] + b) % 2 == 0
        return jnp.where(high, extent - 1, 0)

    def face_open(coords_ref, d, b):
        if b == 0:
            return jnp.bool_(True)
        return jnp.logical_and(coords_ref[d] > 0, coords_ref[d] < sizes[d] - 1)

    def put_faces(read_tile, read_rows, coords_ref, index, outs):
        for (d, b), out in zip(faces, outs):
            if d == 0:
                x = face_position(coords_ref, d, b, X)
                for t in range(T):
                    out[index, pl.ds(t * 8, 8), :] = read_tile(x, t)
            elif d == 1:
                out[index] = read_rows(face_position(coords_ref, d, b, Y))

    def depth_faces(fields, coords_ref, count, addends=2):
        rows_i = lax.broadcasted_iota(jnp.int32, (2 * count, lanes), 0)
        lanes_i = lax.broadcasted_iota(jnp.int32, (2 * count, lanes), 1)
        z = [face_position(coords_ref, 2, b, lanes) for b in range(2)]
        total = jnp.zeros((2 * count, X * Y), F32)
        for f, field in enumerate(fields):
            hit = [
                jnp.logical_and(rows_i == b * count + f, lanes_i == z[b]) for b in range(2)
            ]
            pick = jnp.where(jnp.logical_or(*hit), 1.0, 0.0).astype(BF16)
            for part in halves(field())[:addends]:
                total = total + lax.dot_general(
                    pick,
                    part.astype(BF16),
                    (((1,), (1,)), ((), ())),
                    preferred_element_type=F32,
                )
        return total

    def turned_depth(values):
        return jnp.transpose(jnp.concatenate(halves(values), axis=0)).astype(BF16)

    def spread_depth(turned, coords_ref, rows_of):
        total = turned.shape[1] // 2
        rows_i = lax.broadcasted_iota(jnp.int32, (2 * total, lanes), 0) % total
        lanes_i = lax.broadcasted_iota(jnp.int32, (2 * total, lanes), 1)
        hit = [
            jnp.logical_and(
                rows_i == rows_of[b], lanes_i == face_position(coords_ref, 2, b, lanes)
            )
            for b in range(2)
        ]
        place = jnp.where(jnp.logical_or(*hit), 1.0, 0.0).astype(BF16)
        return jnp.dot(turned, place, preferred_element_type=F32)

    def plain_neighbours(read, x, t):
        sub, _ = iotas()
        tile = read(x, t)
        x_low = read(jnp.maximum(x - 1, 0), t)
        x_high = read(jnp.minimum(x + 1, X - 1), t)
        before = jnp.where(sub == 7, read(x, t - 1), tile) if t > 0 else tile
        after = jnp.where(sub == 0, read(x, t + 1), tile) if t < T - 1 else tile
        return tile, (
            x_low,
            x_high,
            pltpu.roll(before, 1, 0),
            pltpu.roll(after, 7, 0),
            pltpu.roll(tile, 1, 1),
            pltpu.roll(tile, lanes - 1, 1),
        )

    def valid(x, t):
        sub, lane = iotas()
        yes = sub >= 0
        return (
            jnp.logical_and(yes, x > 0),
            jnp.logical_and(yes, x < X - 1),
            sub > 0 if t == 0 else yes,
            sub < 7 if t == T - 1 else yes,
            lane > 0,
            lane < lanes - 1,
        )

    def over_rows(body, group=2):
        def several(i, carry):
            for j in range(group):
                body(i * group + j)
            return carry

        lax.fori_loop(0, X // group, several, 0)

    def face_shape(d, count):
        return ((count, Y, Z), (count, X, Z), (-(-count // 8) * 8, X * Y))[d]

    def face_outs(count):
        return [(face_shape(d, count), F32, VM) for d, _ in faces]

    def exchange(payload):
        received = [None] * len(faces)
        for (d, b), part in zip(faces, payload):
            n = sizes[d]
            swap = [(i, (i + 1 if (i + b) % 2 == 0 else i - 1) % n) for i in range(n)]
            received[faces.index((d, b))] = lax.ppermute(part, AXES[d], swap)
        return received

    def to_owners(rows, sign):
        parts = []
        for shift in range(1, spans):
            part = rows[(shift - 1) * cap : shift * cap]
            parts.append(
                lax.ppermute(
                    part, "span", [(i, (i + sign * shift) % spans) for i in range(spans)]
                )
            )
        return parts[0] if spans == 2 else jnp.concatenate(parts, axis=0)

    def everyone(partial):
        return lax.all_to_all(partial, AXES, split_axis=0, concat_axis=0, tiled=True)

    field_shape = (loads, X * Y, Z)
    plain_shape = (X * Y, Z)
    face_count = len(faces)

    def first_kernel(
        void_hbm, owner_hbm, load_hbm, phase_hbm, blocks_hbm,
        table_ref, far_ref, load_ref, phase_ref, blocks_ref, coords_ref, void_ref,
        owner_ref, arrived,
    ):
        me = lax.axis_index("span")
        copies = [
            pltpu.make_async_copy(source, target, arrived.at[i])
            for i, (source, target) in enumerate(
                (
                    (void_hbm, void_ref),
                    (owner_hbm, owner_ref),
                    (load_hbm, load_ref),
                    (phase_hbm, phase_ref),
                    (blocks_hbm.at[pl.ds(me * cap, cap)], blocks_ref),
                )
            )
        ]
        for copy in copies:
            copy.start()
        for d, axis in enumerate(AXES):
            coords_ref[d] = lax.axis_index(axis)
        for i in range(slots + 1):
            table_ref[i] = -1
        copies[0].wait()
        copies[1].wait()
        used = jnp.int32(0)
        for n in range(bricks):
            at = (n // (bricks_y * bricks_z), n // bricks_z % bricks_y, n % bricks_z)
            solid = 1 - void_ref[at]
            relative = jnp.where(solid == 1, (owner_ref[at] + spans - me) % spans, 0)
            shift = relative * bits
            rank = lax.shift_right_logical(used, shift) & ((1 << bits) - 1)
            index = jnp.where(solid == 1, relative * cap + rank, slots)
            table_ref[index] = n
            used = used + lax.shift_left(solid, shift)
        copies[2].wait()
        gather_bricks(load_ref, table_ref, cap, remote, far_ref, group=8)
        copies[3].wait()
        copies[4].wait()

    table, far, load_f, phase_f, near_blocks, coords, void = pl.pallas_call(
        first_kernel,
        in_specs=[HB] * 5,
        out_specs=[SM, VM, VM, VM, VM, SM, SM],
        out_shape=[
            pltpu.SMEM((slots + 1,), jnp.int32),
            pltpu.VMEM((remote, loads, cells), BF16),
            pltpu.VMEM(field_shape, F32),
            pltpu.VMEM(plain_shape, F32),
            pltpu.VMEM((cap, cells, cells), BF16),
            pltpu.SMEM((3,), jnp.int32),
            pltpu.SMEM(void.shape, jnp.int32),
        ],
        scratch_shapes=[
            pltpu.SMEM(owner.shape, jnp.int32),
            pltpu.SemaphoreType.DMA((5,)),
        ],
        compiler_params=pltpu.CompilerParams(vmem_limit_bytes=12 << 20),
        name="first",
    )(*[
        pltpu.with_memory_space_constraint(a, pltpu.HBM)
        for a in (void, owner, load_f, phase_f, precond)
    ])

    def near_kernel(bring):
        def kernel(table_ref, coords_ref, source_ref, blocks_ref, *refs):
            copies = []
            if bring:
                hbm, field_ref, far_ref, rows_ref, image_ref, split, arrived = refs
                for shift in range(1, spans):
                    source = (coords_ref[0] + spans - shift) % spans
                    copies.append(
                        pltpu.make_async_copy(
                            hbm.at[pl.ds(source * cap, cap)],
                            far_ref.at[pl.ds((shift - 1) * cap, cap)],
                            arrived.at[shift - 1],
                        )
                    )
                    copies[-1].start()
            else:
                field_ref, rows_ref, image_ref, split = refs
            field_ref[...] = jnp.zeros(field_ref.shape, F32)
            gather_bricks(source_ref, table_ref, 0, cap, rows_ref)
            for r in range(cap):
                image_ref[r] = jnp.dot(
                    rows_ref[r], blocks_ref[r], preferred_element_type=F32
                )
            scatter_bricks(field_ref, table_ref, 0, cap, image_ref, split)
            for copy in copies:
                copy.wait()

        return kernel

    def near_part(source, bring):
        ins = [(table, SM), (coords, SM), (source, VM), (near_blocks, VM)]
        outs = [(field_shape, F32, VM)]
        scratch = [
            pltpu.VMEM((cap, loads, cells), BF16),
            pltpu.VMEM((cap, loads, cells), F32),
            pltpu.VMEM((cap, 2, loads, cells), F32),
        ]
        if bring:
            ins.append((precond, HB))
            outs.append(((remote, cells, cells), BF16, VM))
            scratch.append(pltpu.SemaphoreType.DMA((spans - 1,)))
        return call(near_kernel(bring), ins, outs, scratch=scratch, flops=8000000000)

    def blocks_kernel(rows_ref, blocks_ref, out_ref):
        for r in range(remote):
            out_ref[r] = jnp.dot(
                rows_ref[r], blocks_ref[r], preferred_element_type=F32
            ).astype(out_ref.dtype)

    def far_part(rows, dtype):
        (image,) = call(
            blocks_kernel,
            [(to_owners(rows, 1), VM), (far_blocks, VM)],
            [((remote, loads, cells), dtype, VM)],
        )
        return to_owners(image, -1)

    def faces_kernel(extra):
        def kernel(table_ref, coords_ref, image_ref, begun_ref, *refs):
            extras = refs[:extra]
            field_ref = refs[extra]
            outs = refs[extra + 1 : extra + 1 + face_count]
            split = refs[extra + 1 + face_count]
            scatter_bricks(field_ref, table_ref, cap, remote, image_ref, split)
            for l in range(loads):
                put_faces(
                    lambda x, t: field_ref[l, row(x, t), :],
                    lambda y: field_ref[l, pl.ds(y, X, stride=Y), :],
                    coords_ref, l, outs,
                )
            for e in range(extra):
                ref = extras[e]
                put_faces(
                    lambda x, t: ref[row(x, t), :],
                    lambda y: ref[pl.ds(y, X, stride=Y), :],
                    coords_ref, loads + e, outs,
                )
            count = outs[-1].shape[0]
            depth = depth_faces(
                [lambda l=l: field_ref[l] for l in range(loads)]
                + [lambda e=e: extras[e][...] for e in range(extra)],
                coords_ref, count, addends=1,
            )
            for (d, b), out in zip(faces, outs):
                if d == 2:
                    out[...] = depth[b * count : (b + 1) * count]

        return kernel

    def to_field(begun, image, extras):
        result = call(
            faces_kernel(len(extras)),
            [(table, SM), (coords, SM), (image, VM), (begun, VM)]
            + [(e, VM) for e in extras],
            [(field_shape, F32, VM)] + face_outs(loads + len(extras)),
            scratch=[pltpu.VMEM((remote, 2, loads, cells), F32)],
            aliases={3: 0},
        )
        return result[0], result[1:], exchange(result[1:])

    def stiffness_kernel(void_ref, phase_ref, ks_ref):
        _, lane = iotas()
        for bx in range(bricks_x):
            for by in range(bricks_y):
                mask = jnp.zeros((8, lanes), F32)
                for bz in range(bricks_z):
                    solid = 1 - void_ref[bx, by, bz]
                    mask = jnp.where((lane >> 3) == bz, solid.astype(F32), mask)
                for i in range(BE):
                    at = row(bx * BE + i, by)
                    p = phase_ref[at, :]
                    stiffness = void_stiffness + (1.0 - void_stiffness) * (p * p * p)
                    ks_ref[at, :] = mask * stiffness

    begun, far_blocks = near_part(load_f, True)
    far_image = far_part(far, F32)
    (ks,) = call(
        stiffness_kernel, [(void, SM), (phase_f, VM)], [(plain_shape, F32, VM)],
        flops=2000000000,
    )
    z_field, z_sent, z_halo = to_field(begun, far_image, [ks, phase_f])

    def joined(mine, other):
        both = jnp.logical_and(mine > 0.0, other > 0.0)
        return jnp.where(both, 0.5 * (mine + other), 0.0)

    def inner_kernel(z_ref, load_ref, ks_ref, phase_ref, q_ref, weight_ref, start_ref, dots_ref):
        dots_ref[...] = jnp.zeros(dots_ref.shape, F32)

        def body(x):
            for t in range(T):
                at = row(x, t)
                inside = valid(x, t)
                ks_tile, ks_near = plain_neighbours(lambda x, t: ks_ref[row(x, t), :], x, t)
                p, p_near = plain_neighbours(lambda x, t: phase_ref[row(x, t), :], x, t)
                around = jnp.zeros((8, lanes), F32)
                for d in range(6):
                    around = around + jnp.where(inside[d], p_near[d], 0.0)
                start_ref[at, :] = (
                    p / time_step
                    - 0.5 * p * (1.0 - p) * (1.0 - 2.0 * p)
                    + interface_weight * around
                ) * inverse
                total = jnp.where(ks_tile > 0.0, spring_rate, 0.0)
                weights = []
                for d in range(6):
                    weight = jnp.where(inside[d], joined(ks_tile, ks_near[d]), 0.0)
                    weights.append(weight)
                    weight_ref[d, at, :] = weight
                    total = total + weight
                for l in range(loads):
                    tile, near_tiles = plain_neighbours(
                        lambda x, t: z_ref[l, row(x, t), :], x, t
                    )
                    image = total * tile
                    for d in range(6):
                        image = image - weights[d] * near_tiles[d]
                    q_ref[l, at, :] = image
                    dots_ref[0, l] += load_ref[l, at, :] * tile
                    dots_ref[1, l] += image * tile

        over_rows(body)

    q_inner, weights, start_inner, dots = call(
        inner_kernel,
        [(z_field, VM), (load_f, VM), (ks, VM), (phase_f, VM)],
        [
            (field_shape, F32, VM),
            ((6, X * Y, Z), F32, VM),
            (plain_shape, F32, VM),
            ((2, loads, 8, Z), F32, VM),
        ],
        flops=8000000000,
    )

    def face_weight(coords_ref, d, b, sent, received, at):
        other = jnp.where(face_open(coords_ref, d, b), received[at], 0.0)
        return joined(sent[at], other)

    def row_pieces(d):
        return [pl.ds(i * 8, 8) for i in range((Y if d == 0 else X) // 8)]

    def edges_kernel(coords_ref, table_ref, q_in, start_in, dots_in, *refs):
        sent = refs[:face_count]
        received = refs[face_count : 2 * face_count]
        q_ref, start_ref, dots_ref, far_ref = refs[2 * face_count : 2 * face_count + 4]
        moved = refs[2 * face_count + 4 :]
        scale = interface_weight * inverse
        for (d, b), mine, other, shift in zip(faces, sent, received, moved):
            is_open = face_open(coords_ref, d, b)
            if d < 2:
                for at in row_pieces(d):
                    weight = face_weight(coords_ref, d, b, mine, other, (loads, at))
                    for l in range(loads):
                        tile = mine[l, at, :]
                        change = weight * (tile - other[l, at, :])
                        shift[l, at, :] = change
                        dots_ref[1, l] += tile * change
                    shift[loads, at, :] = jnp.where(
                        is_open, scale * other[loads + 1, at, :], 0.0
                    )
                for l in range(loads + 1):
                    target = q_ref.at[l] if l < loads else start_ref
                    if d == 0:
                        x = face_position(coords_ref, d, b, X)
                        for t in range(T):
                            target[row(x, t), :] += shift[l, pl.ds(t * 8, 8), :]
                    else:
                        y = face_position(coords_ref, d, b, Y)
                        at = pl.ds(y, X, stride=Y)
                        target[at, :] = target[at, :] + shift[l]
            else:
                weight = face_weight(coords_ref, d, b, mine, other, (pl.ds(loads, 1), slice(None)))
                tile = mine[pl.ds(0, loads), :]
                change = weight * (tile - other[pl.ds(0, loads), :])
                shift[pl.ds(0, loads), :] = change
                shift[pl.ds(loads, 8), :] = jnp.zeros((8, X * Y), F32)
                shift[pl.ds(loads, 1), :] = jnp.where(
                    is_open, scale * other[pl.ds(loads + 1, 1), :], 0.0
                )
                product = tile * change
                eight = sum(
                    product[:, i * lanes : (i + 1) * lanes] for i in range(X * Y // lanes)
                )
                sub, _ = iotas()
                for l in range(loads):
                    dots_ref[1, l] += jnp.where(sub == l, eight, 0.0)
        depth = [shift for (d, _), shift in zip(faces, moved) if d == 2]
        turned = turned_depth(jnp.concatenate([ref[...] for ref in depth], axis=0))
        for l in range(loads + 1):
            target = q_ref.at[l] if l < loads else start_ref
            target[...] = target[...] + spread_depth(
                turned, coords_ref, (l, depth[0].shape[0] + l)
            )
        gather_bricks(q_ref, table_ref, cap, remote, far_ref)

    q_field, start, dots, far = call(
        edges_kernel,
        [(coords, SM), (table, SM), (q_inner, VM), (start_inner, VM), (dots, VM)]
        + [(a, VM) for a in z_sent]
        + [(a, VM) for a in z_halo],
        [
            (field_shape, F32, VM),
            (plain_shape, F32, VM),
            ((2, loads, 8, Z), F32, VM),
            ((remote, loads, cells), BF16, VM),
        ],
        scratch=[pltpu.VMEM(face_shape(d, loads + 1), F32) for d, _ in faces],
        aliases={2: 0, 3: 1, 4: 2},
    )

    far_image = far_part(far, BF16)
    w_field, w_sent, w_halo = to_field(near_part(q_field, False)[0], far_image, [start])

    products = 5

    def more_kernel(w_ref, q_ref, load_ref, weight_ref, ks_ref, more_ref):
        more_ref[...] = jnp.zeros(more_ref.shape, F32)

        def body(x):
            for t in range(T):
                at = row(x, t)
                weights = [weight_ref[d, at, :] for d in (1, 3, 5)]
                spring = jnp.where(ks_ref[at, :] > 0.0, spring_rate, 0.0)
                for l in range(loads):
                    tile, near_tiles = plain_neighbours(
                        lambda x, t: w_ref[l, row(x, t), :], x, t
                    )
                    energy = spring * tile * tile
                    for weight, d in zip(weights, (1, 3, 5)):
                        gap = tile - near_tiles[d]
                        energy = energy + weight * gap * gap
                    more_ref[0, l] += load_ref[l, at, :] * tile
                    more_ref[1, l] += q_ref[l, at, :] * tile
                    more_ref[2, l] += energy

        over_rows(body)

    (more,) = call(
        more_kernel,
        [(w_field, VM), (q_field, VM), (load_f, VM), (weights, VM), (ks, VM)],
        [((3, loads, 8, Z), F32, VM)],
        flops=8000000000,
    )

    def total_kernel(coords_ref, dots_ref, more_in, *refs):
        z_mine = refs[:face_count]
        z_other = refs[face_count : 2 * face_count]
        w_mine = refs[2 * face_count : 3 * face_count]
        w_other = refs[3 * face_count : 4 * face_count]
        out_ref, more_ref = refs[4 * face_count : 4 * face_count + 2]
        gaps = refs[4 * face_count + 2 : 5 * face_count + 2]
        starts = refs[5 * face_count + 2 :]
        sub, lane = iotas()
        for (d, b), z_a, z_b, w_a, w_b, gap, begin in zip(
            faces, z_mine, z_other, w_mine, w_other, gaps, starts
        ):
            if d < 2:
                begin[...] = w_b[loads]
                for at in row_pieces(d):
                    weight = face_weight(coords_ref, d, b, z_a, z_b, (loads, at))
                    solid = weight > 0.0
                    for l in range(loads):
                        tile = w_a[l, at, :]
                        between = tile - w_b[l, at, :]
                        more_ref[2, l] += weight * tile * between
                        gap[1, l, at, :] = jnp.where(solid, between, 0.0)
                        gap[0, l, at, :] = jnp.where(
                            solid, z_a[l, at, :] - z_b[l, at, :], 0.0
                        )
            else:
                begin[...] = w_b[pl.ds(loads, 8), :]
                weight = face_weight(coords_ref, d, b, z_a, z_b, (pl.ds(loads, 1), slice(None)))
                solid = weight > 0.0
                tile = w_a[pl.ds(0, loads), :]
                between = tile - w_b[pl.ds(0, loads), :]
                product = weight * tile * between
                gap[1] = jnp.where(solid, between, 0.0)
                gap[0] = jnp.where(
                    solid, z_a[pl.ds(0, loads), :] - z_b[pl.ds(0, loads), :], 0.0
                )
                eight = sum(
                    product[:, i * lanes : (i + 1) * lanes] for i in range(X * Y // lanes)
                )
                for l in range(loads):
                    more_ref[2, l] += jnp.where(sub == l, eight, 0.0)
        result = jnp.zeros((1, lanes), F32)
        lane1 = lane[:1]
        for k in range(products):
            for l in range(loads):
                part = dots_ref[k, l] if k < 2 else more_ref[k - 2, l]
                value = jnp.sum(jnp.sum(part, axis=0, keepdims=True), axis=1, keepdims=True)
                result = jnp.where(lane1 == k * loads + l, value, result)
        out_ref[...] = jnp.broadcast_to(result, (devices, lanes))

    partial, _, *kept = call(
        total_kernel,
        [(coords, SM), (dots, VM), (more, VM)]
        + [(a, VM) for part in (z_sent, z_halo, w_sent, w_halo) for a in part],
        [((devices, lanes), F32, VM), ((3, loads, 8, Z), F32, VM)]
        + [((2,) + face_shape(d, loads), F32, VM) for d, _ in faces]
        + [((8, X * Y) if d == 2 else face_shape(d, 1)[1:], F32, VM) for d, _ in faces],
        aliases={2: 1},
    )
    gaps, start_halo = kept[:face_count], kept[face_count:]
    sums = everyone(partial)

    def device_beyond(coords_ref, d, b):
        place = [coords_ref[i] for i in range(3)]
        step = jnp.where((place[d] + b) % 2 == 0, 1, -1)
        place[d] = jnp.where(face_open(coords_ref, d, b), place[d] + step, place[d])
        return (place[0] * sizes[1] + place[1]) * sizes[2] + place[2]

    face_rows = max(X, Y)
    message = face_rows + 1

    def solve_kernel(
        coords_ref, sums_ref, ks_ref, phase_ref, z_ref, w_ref, *refs
    ):
        gap_refs = refs[:face_count]
        sens_ref, out_ref, x_hbm, x_ref, plain_ref, link_ref, held_ref, written = refs[
            face_count:
        ]
        sub, lane = iotas()
        total = jnp.broadcast_to(
            jnp.sum(sums_ref[...], axis=0, keepdims=True), (8, lanes)
        )
        bz, zq, bw, qw, ws = [
            pltpu.roll(total, (lanes - k * loads) % lanes, 1) for k in range(products)
        ]
        alpha = bz / zq
        bz_next = bz - alpha * (bw + zq) + alpha * alpha * qw
        beta = bz_next / bz
        grow = 1.0 + beta
        curvature = grow * grow * zq - 2.0 * grow * alpha * qw + alpha * alpha * ws
        alpha_next = bz_next / curvature
        for_z = alpha + alpha_next * grow
        for_w = -alpha_next * alpha
        c_z = [jnp.broadcast_to(for_z[0:1, l : l + 1], (8, lanes)) for l in range(loads)]
        c_w = [jnp.broadcast_to(for_w[0:1, l : l + 1], (8, lanes)) for l in range(loads)]
        writes = []
        for l in range(loads):
            for i in range(tiles):
                at = pl.ds(i * 8, 8)
                x_ref[l, at, :] = c_z[l] * z_ref[l, at, :] + c_w[l] * w_ref[l, at, :]
            writes.append(
                pltpu.make_async_copy(x_ref.at[l], x_hbm.at[l], written.at[l])
            )
            writes[-1].start()

        def body(x):
            for t in range(T):
                at = row(x, t)
                inside = valid(x, t)
                ks_tile, ks_near = plain_neighbours(lambda x, t: ks_ref[row(x, t), :], x, t)
                gaps_of = [jnp.zeros((8, lanes), F32) for _ in range(3)]
                for l in range(loads):
                    tile, near_tiles = plain_neighbours(
                        lambda x, t: x_ref[l, row(x, t), :], x, t
                    )
                    for d in range(3):
                        gap = tile - near_tiles[2 * d + 1]
                        gaps_of[d] = gaps_of[d] + gap * gap
                for d in range(3):
                    n = 2 * d + 1
                    solid = jnp.logical_and(inside[n], joined(ks_tile, ks_near[n]) > 0.0)
                    link_ref[d, at, :] = jnp.where(solid, gaps_of[d], 0.0)

        over_rows(body)
        for x in range(X):
            for t in range(T):
                at = row(x, t)
                along_y = link_ref[1, at, :]
                before = link_ref[1, row(x, t - 1), :] if t > 0 else 0.0
                along_z = link_ref[2, at, :]
                energy = link_ref[0, at, :] + along_y + along_z
                energy = energy + pltpu.roll(jnp.where(sub == 7, before, along_y), 1, 0)
                energy = energy + pltpu.roll(along_z, 1, 1)
                if x > 0:
                    energy = energy + link_ref[0, row(x - 1, t), :]
                plain_ref[at, :] = energy
        held_ref[...] = jnp.zeros(held_ref.shape, F32)
        for (d, b), between in zip(faces, gap_refs):
            if d < 2:
                pieces = []
                for at in row_pieces(d):
                    energy = jnp.zeros((8, lanes), F32)
                    for l in range(loads):
                        gap = c_z[l] * between[0, l, at, :] + c_w[l] * between[1, l, at, :]
                        energy = energy + gap * gap
                    pieces.append(energy)
                if d == 0:
                    x = face_position(coords_ref, d, b, X)
                    for t in range(T):
                        plain_ref[row(x, t), :] += pieces[t]
                else:
                    at = pl.ds(face_position(coords_ref, d, b, Y), X, stride=Y)
                    plain_ref[at, :] = plain_ref[at, :] + jnp.concatenate(pieces, axis=0)
            else:
                by_z = jnp.concatenate([c[0:1, :1] for c in c_z], axis=0)
                by_w = jnp.concatenate([c[0:1, :1] for c in c_w], axis=0)
                gap = by_z * between[0] + by_w * between[1]
                held_ref[pl.ds(b, 1), :] = jnp.sum(gap * gap, axis=0, keepdims=True)
        spread = spread_depth(turned_depth(held_ref[...]), coords_ref, (0, 1))
        energy = plain_ref[...] + spread
        p = phase_ref[...]
        negative = 1.5 * (1.0 - void_stiffness) * (p * p) * energy
        sens_ref[...] = -negative
        peak = jnp.max(jnp.max(negative, axis=0, keepdims=True), axis=1, keepdims=True)
        peak = jnp.broadcast_to(peak, (1, lanes))
        high, rest = halves(peak)
        middle, low = halves(rest)
        lane1 = lane[:1]
        tail = jnp.where(lane1 == 0, high, jnp.where(lane1 == 1, middle, low)).astype(BF16)
        for i in range(devices):
            out_ref[i, pl.ds(face_rows, 1), :] = tail
        depth = depth_faces([lambda: sens_ref[...]], coords_ref, 8, addends=1)
        for d, b in faces:
            @pl.when(face_open(coords_ref, d, b))
            def _(d=d, b=b):
                to = device_beyond(coords_ref, d, b)
                if d == 0:
                    x = face_position(coords_ref, d, b, X)
                    value = sens_ref[pl.ds(pl.multiple_of(x * Y, 8), Y), :]
                elif d == 1:
                    value = sens_ref[
                        pl.ds(face_position(coords_ref, d, b, Y), X, stride=Y), :
                    ]
                else:
                    value = jnp.concatenate(
                        [
                            depth[b * 8 : b * 8 + 1, i * lanes : (i + 1) * lanes]
                            for i in range(X * Y // lanes)
                        ],
                        axis=0,
                    )
                out_ref[to, pl.ds(0, value.shape[0]), :] = value.astype(BF16)
        for write in writes:
            write.wait()

    sens_field, outgoing, displacement = call(
        solve_kernel,
        [
            (coords, SM), (sums, VM), (ks, VM), (phase_f, VM), (z_field, VM),
            (w_field, VM),
        ]
        + [(a, VM) for a in gaps],
        [
            (plain_shape, F32, VM),
            ((devices, message, lanes), BF16, VM),
            (field_shape, F32, HB),
        ],
        scratch=[
            pltpu.VMEM(field_shape, F32),
            pltpu.VMEM(plain_shape, F32),
            pltpu.VMEM((3,) + plain_shape, F32),
            pltpu.VMEM((8, X * Y), F32),
            pltpu.SemaphoreType.DMA((loads,)),
        ],
    )
    incoming = everyone(outgoing)

    def sweep_kernel(coords_ref, in_ref, sens_ref, start_ref, phase_ref, *refs):
        starts = refs[:face_count]
        out_hbm, sens_hbm, out_ref, once_ref, held_ref, written = refs[face_count:]
        writes = [pltpu.make_async_copy(sens_ref, sens_hbm, written.at[2])]
        writes[0].start()
        sub, lane = iotas()
        tails = in_ref[:, pl.ds(face_rows, 1), :].astype(F32)
        tails = tails.reshape(devices, lanes)
        peaks = tails + pltpu.roll(tails, lanes - 1, 1) + pltpu.roll(tails, lanes - 2, 1)
        peak = jnp.max(peaks, axis=0, keepdims=True)[:, :1]
        scale1 = jnp.broadcast_to(1.0 / (peak + epsilon_peak), (1, lanes))
        scale = jnp.broadcast_to(scale1, (8, lanes))
        for i in range(tiles):
            at = pl.ds(i * 8, 8)
            once_ref[at, :] = start_ref[at, :] - inverse * (sens_ref[at, :] * scale)

        held_ref[...] = jnp.zeros(held_ref.shape, F32)
        factor = interface_weight * inverse
        edges = []
        for (d, b), start_b in zip(faces, starts):
            is_open = face_open(coords_ref, d, b)
            source = device_beyond(coords_ref, d, b)
            sent = in_ref[source].astype(F32)
            if d < 2:
                value = start_b[...] - (inverse * scale1) * sent[: (Y if d == 0 else X)]
                value = jnp.where(is_open, factor * value, 0.0)
                if d == 0:
                    x = face_position(coords_ref, d, b, X)
                    at = pl.ds(pl.multiple_of(x * Y, 8), Y)
                else:
                    at = pl.ds(face_position(coords_ref, d, b, Y), X, stride=Y)
                edges.append((at, value))
            else:
                for i in range(X * Y // lanes):
                    at = pl.ds(i * lanes, lanes)
                    value = start_b[pl.ds(0, 1), at] - (inverse * scale1) * sent[i : i + 1]
                    held_ref[pl.ds(b, 1), at] = jnp.where(is_open, factor * value, 0.0)
        out_ref[...] = spread_depth(turned_depth(held_ref[...]), coords_ref, (0, 1))
        for at, value in edges:
            out_ref[at, :] = out_ref[at, :] + value

        def body(x):
            for t in range(T):
                at = row(x, t)
                inside = valid(x, t)
                _, near_tiles = plain_neighbours(lambda x, t: once_ref[row(x, t), :], x, t)
                around = jnp.zeros((8, lanes), F32)
                for d in range(6):
                    around = around + jnp.where(inside[d], near_tiles[d], 0.0)
                p = phase_ref[at, :]
                drive = (
                    p / time_step
                    - 0.5 * p * (1.0 - p) * (1.0 - 2.0 * p)
                    - sens_ref[at, :] * scale
                )
                out_ref[at, :] += (drive + interface_weight * around) * inverse

        half = X // 2
        for part in range(2):
            for x in range(part * half, (part + 1) * half):
                body(x)
            at = pl.ds(part * half * Y, half * Y)
            writes.append(
                pltpu.make_async_copy(out_ref.at[at], out_hbm.at[at], written.at[part])
            )
            writes[-1].start()
        for write in writes:
            write.wait()

    phase_next, sensitivity = call(
        sweep_kernel,
        [(coords, SM), (incoming, VM), (sens_field, VM), (start, VM), (phase_f, VM)]
        + [(a, VM) for a in start_halo],
        [(plain_shape, F32, HB), (plain_shape, F32, HB)],
        scratch=[
            pltpu.VMEM(plain_shape, F32),
            pltpu.VMEM(plain_shape, F32),
            pltpu.VMEM((8, X * Y), F32),
            pltpu.SemaphoreType.DMA((3,)),
        ],
    )
    return (
        displacement.reshape(load.shape),
        sensitivity.reshape(phase.shape),
        phase_next.reshape(phase.shape),
    )


def solution(mesh):
    return program(mesh)


def program(mesh):
    return jax.shard_map(
        local,
        mesh=mesh,
        in_specs=(
            P(None, "span", "height", "depth"),
            P("span", "height", "depth"),
            P("span", "height", "depth"),
            P("span", "height", "depth"),
            P(("span", "height", "depth"), None, None),
        ),
        out_specs=(
            P(None, "span", "height", "depth"),
            P("span", "height", "depth"),
            P("span", "height", "depth"),
        ),
        check_vma=False,
    )
```

profile of v0, /device:TPU:0, one launch (start us, length us, event | category | flops | bytes accessed | tf_op | source)
XLA Modules:
  0.0 70.6 jit_solution(12548487252041100235)
XLA Ops:
  0.6 2.6 %first.1 = (s32[17]{0:T(128)S(4)}, bf16[8,8,512]{2,1,0:T(8,128)(2,1)S(1)}, f32[8,256,128]{2,1,0:T(8,128)S(1)}, f32[256,128]{1,0:T(8,128)S(1)}, bf16[8,512,512]{2...) custom-call(s32[2,2,16]{2,1,0:T(2,128)} %void_hbm.1, s32[2,2,16]{2,1,0:T(2,128)} %owner_hbm.1, ...), custom_call_target="tpu_custom_call" | custom-call | tf_op jit(solution)/shard_map/first/pallas_call | solution.py:365
  3.3 3.1 %collective-permute-start = (bf16[8,8,512]{2,1,0:T(8,128)(2,1)S(1)}, bf16[8,8,512]{2,1,0:T(8,128)(2,1)S(1)}, u32[]{:S(2)}, u32[]{:S(2)}) collective-permute-start(bf16[8,8,512]{2,1,0:T(8,128)(2,1)S(1)} %get-tuple-element.50), channel_id=1, source_target_pairs={{0,16},{16,0},{1,17},{17,1},{2,18},{18,2},{3,19},{19,3},{4,20},{20... | collective-permute-start | bytes 196616 | tf_op jit(solution)/shard_map/ppermute | solution.py:311
  6.3 3.0 %shard_map.76 = (f32[8,256,128]{2,1,0:T(8,128)S(1)}, bf16[8,512,512]{2,1,0:T(8,128)(2,1)S(1)}) custom-call(s32[17]{0:T(128)S(4)} %get-tuple-element.49.table_ref, s32[3]{0:T(128)S(4)} %get-tuple-element.48.coords_ref, f32[8,256,128]{2,1,0:T(8,128)S(1)} %get-tuple-element.51.source_ref.load_ref, bf16[8,512,512]{2,1,0:T(8,128)(2,1)S(1)} %get-tuple-element.52.blocks_ref, ...), custom_call_target="tpu_custom_call" | custom-call | flops 8000000000 | bytes 1048576 | tf_op jit(solution)/shard_map/pallas_call | solution.py:35
  9.3 0.0 collective-permute-done.rows_ref
  9.3 0.6 shard_map.77
  10.0 1.3 %collective-permute-start.1 = (f32[8,8,512]{2,1,0:T(8,128)S(1)}, f32[8,8,512]{2,1,0:T(8,128)S(1)}, u32[]{:S(2)}, u32[]{:S(2)}) collective-permute-start(f32[8,8,512]{2,1,0:T(8,128)S(1)} %shard_map.77), channel_id=1, source_target_pairs={{0,16},{16,0},{1,17},{17,1},{2,18},{18,2},{3,19},{19,3},{4,20},{20... | collective-permute-start | bytes 393224 | tf_op jit(solution)/shard_map/ppermute | solution.py:311
  11.2 0.1 shard_map.78.refs_0_.ks_ref
  11.3 3.6 %collective-permute-done.1.image_ref = f32[8,8,512]{2,1,0:T(8,128)S(1)} collective-permute-done((f32[8,8,512]{2,1,0:T(8,128)S(1)}, f32[8,8,512]{2,1,0:T(8,128)S(1)}, u32[]{:S(2)}, u32[]{:S(2)}) %collective-permute-start.1) | collective-permute-done | bytes 131104 | tf_op jit(solution)/shard_map/ppermute | solution.py:311
  14.9 1.1 %shard_map.79 = (f32[8,256,128]{2,1,0:T(8,128)S(1)}, f32[10,16,128]{2,1,0:T(8,128)S(1)}, f32[10,16,128]{2,1,0:T(8,128)S(1)}, f32[10,16,128]{2,1,0:T(8,128)S(1)},...) custom-call(s32[17]{0:T(128)S(4)} %get-tuple-element.49.table_ref, ...), custom_call_target="tpu_custom_call", output_to_operand_aliasing={{0}: (3, {})} | custom-call | bytes 1048576 | tf_op jit(solution)/shard_map/pallas_call | solution.py:35
  16.1 1.6 %collective-permute-start.5 = (f32[16,256]{1,0:T(8,128)S(1)}, f32[16,256]{1,0:T(8,128)S(1)}, u32[]{:S(2)}, u32[]{:S(2)}) collective-permute-start(f32[16,256]{1,0:T(8,128)S(1)} %get-tuple-element.64.refs_3_), channel_id=1, source_target_pairs={{0,1},{1,0},{2,3},{3,2},{4,5},{5,4},{6,7},{7,6},{8,9},{9,8},{10,11... | collective-permute-start | bytes 49160 | tf_op jit(solution)/shard_map/ppermute | solution.py:303
  17.7 2.5 %collective-permute-start.6 = (f32[16,256]{1,0:T(8,128)S(1)}, f32[16,256]{1,0:T(8,128)S(1)}, u32[]{:S(2)}, u32[]{:S(2)}) collective-permute-start(f32[16,256]{1,0:T(8,128)S(1)} %get-tuple-element.65.refs_4_), channel_id=1, source_target_pairs={{0,3},{1,2},{2,1},{3,0},{4,7},{5,6},{6,5},{7,4},{8,11},{9,10},{10,... | collective-permute-start | bytes 49160 | tf_op jit(solution)/shard_map/ppermute | solution.py:303
  20.2 1.3 %collective-permute-start.2 = (f32[10,16,128]{2,1,0:T(8,128)S(1)}, f32[10,16,128]{2,1,0:T(8,128)S(1)}, u32[]{:S(2)}, u32[]{:S(2)}) collective-permute-start(f32[10,16,128]{2,1,0:T(8,128)S(1)} %get-tuple-element.61.refs_0_), channel_id=1, source_target_pairs={{0,16},{16,0},{1,17},{17,1},{2,18},{18,2},{3,19},{19,3},{4,20},{20... | collective-permute-start | bytes 245768 | tf_op jit(solution)/shard_map/ppermute | solution.py:303
  21.4 0.0 collective-permute-start.3
  21.4 1.6 %collective-permute-start.4 = (f32[10,16,128]{2,1,0:T(8,128)S(1)}, f32[10,16,128]{2,1,0:T(8,128)S(1)}, u32[]{:S(2)}, u32[]{:S(2)}) collective-permute-start(f32[10,16,128]{2,1,0:T(8,128)S(1)} %get-tuple-element.63.refs_2_), channel_id=1, source_target_pairs={{0,12},{4,8},{8,4},{12,0},{1,13},{5,9},{9,5},{13,1},{2,14},{6,10},... | collective-permute-start | bytes 245768 | tf_op jit(solution)/shard_map/ppermute | solution.py:303
  23.0 1.3 %shard_map.80 = (f32[8,256,128]{2,1,0:T(8,128)S(1)}, f32[6,256,128]{2,1,0:T(8,128)S(1)}, f32[256,128]{1,0:T(8,128)S(1)}, f32[2,8,8,128]{3,2,1,0:T(8,128)S(1)}) custom-call(f32[8,256,128]{2,1,0:T(8,128)S(1)} %get-tuple-element.57.z_ref, f32[8,256,128]{2,1,0:T(8,128)S(1)} %get-tuple-element.51.source_ref.load_ref, f32[256,128]{1,0:T(8,128)S(1)} %shard_map.78.refs_0_.ks_ref, ...), custom_call_target="tpu_custom_call" | custom-call | flops 8000000000 | bytes 1048576 | tf_op jit(solution)/shard_map/pallas_call | solution.py:35
  24.4 0.0 collective-permute-done.5.refs_8_
  24.4 0.0 collective-permute-done.6.refs_9_
  24.4 0.2 collective-permute-done.2.refs_5_
  24.6 0.0 collective-permute-done.3.refs_6_
  24.6 0.9 %collective-permute-done.4.refs_7_ = f32[10,16,128]{2,1,0:T(8,128)S(1)} collective-permute-done((f32[10,16,128]{2,1,0:T(8,128)S(1)}, f32[10,16,128]{2,1,0:T(8,128)S(1)}, u32[]{:S(2)}, u32[]{:S(2)}) %collective-permute-start.4) | collective-permute-done | bytes 81952 | tf_op jit(solution)/shard_map/ppermute | solution.py:303
  25.5 2.1 %shard_map.81 = (f32[8,256,128]{2,1,0:T(8,128)S(1)}, f32[256,128]{1,0:T(8,128)S(1)}, f32[2,8,8,128]{3,2,1,0:T(8,128)S(1)}, bf16[8,8,512]{2,1,0:T(8,128)(2,1)S(1)}) custom-call(s32[3]{0:T(128)S(4)} %get-tuple-element.48.coords_ref, s32[17]{0:T(128)S(4)} %get-tuple-element.49.table_ref, ...), custom_call_target="tpu_custom_call", output_to_operand_aliasing={{0}: (2, {}), {1}: (3, {}), {2}: (4, {})} | custom-call | bytes 1048576 | tf_op jit(solution)/shard_map/pallas_call | solution.py:35
  27.6 0.8 %collective-permute-start.7 = (bf16[8,8,512]{2,1,0:T(8,128)(2,1)S(1)}, bf16[8,8,512]{2,1,0:T(8,128)(2,1)S(1)}, u32[]{:S(2)}, u32[]{:S(2)}) collective-permute-start(bf16[8,8,512]{2,1,0:T(8,128)(2,1)S(1)} %get-tuple-element.67), channel_id=1, source_target_pairs={{0,16},{16,0},{1,17},{17,1},{2,18},{18,2},{3,19},{19,3},{4,20},{20... | collective-permute-start | bytes 196616 | tf_op jit(solution)/shard_map/ppermute | solution.py:311
  28.3 3.8 %collective-permute-done.7.rows_ref = bf16[8,8,512]{2,1,0:T(8,128)(2,1)S(1)} collective-permute-done((bf16[8,8,512]{2,1,0:T(8,128)(2,1)S(1)}, bf16[8,8,512]{2,1,0:T(8,128)(2,1)S(1)}, u32[]{:S(2)}, u32[]{:S(2)}) %collective-permute-start.7) | collective-permute-done | bytes 65568 | tf_op jit(solution)/shard_map/ppermute | solution.py:311
  32.1 0.6 shard_map.82
  32.7 0.8 %collective-permute-start.8 = (bf16[8,8,512]{2,1,0:T(8,128)(2,1)S(1)}, bf16[8,8,512]{2,1,0:T(8,128)(2,1)S(1)}, u32[]{:S(2)}, u32[]{:S(2)}) collective-permute-start(bf16[8,8,512]{2,1,0:T(8,128)(2,1)S(1)} %shard_map.82), channel_id=1, source_target_pairs={{0,16},{16,0},{1,17},{17,1},{2,18},{18,2},{3,19},{19,3},{4,20},{20... | collective-permute-start | bytes 196616 | tf_op jit(solution)/shard_map/ppermute | solution.py:311
  33.5 3.0 %shard_map.83.begun_ref = f32[8,256,128]{2,1,0:T(8,128)S(1)} custom-call(s32[17]{0:T(128)S(4)} %get-tuple-element.49.table_ref, s32[3]{0:T(128)S(4)} %get-tuple-element.48.coords_ref, f32[8,256,128]{2,1,0:T(8,128)S(1)} %get-tuple-element.68.source_ref.q_ref, bf16[8,512,512]{2,1,0:T(8,128)(2,1)S(1)} %get-tuple-element.52.blocks_ref), custom_call_target="tpu_custom_call" | custom-call | flops 8000000000 | bytes 1048576 | tf_op jit(solution)/shard_map/pallas_call | solution.py:35
  36.5 0.5 collective-permute-done.8.image_ref
  37.0 1.0 %shard_map.84 = (f32[8,256,128]{2,1,0:T(8,128)S(1)}, f32[9,16,128]{2,1,0:T(8,128)S(1)}, f32[9,16,128]{2,1,0:T(8,128)S(1)}, f32[9,16,128]{2,1,0:T(8,128)S(1)}, f3...) custom-call(s32[17]{0:T(128)S(4)} %get-tuple-element.49.table_ref, ...), custom_call_target="tpu_custom_call", output_to_operand_aliasing={{0}: (3, {})} | custom-call | bytes 1048576 | tf_op jit(solution)/shard_map/pallas_call | solution.py:35
  38.1 0.8 %collective-permute-start.12 = (f32[16,256]{1,0:T(8,128)S(1)}, f32[16,256]{1,0:T(8,128)S(1)}, u32[]{:S(2)}, u32[]{:S(2)}) collective-permute-start(f32[16,256]{1,0:T(8,128)S(1)} %get-tuple-element.75.refs_13_), channel_id=1, source_target_pairs={{0,1},{1,0},{2,3},{3,2},{4,5},{5,4},{6,7},{7,6},{8,9},{9,8},{10,11... | collective-permute-start | bytes 49160 | tf_op jit(solution)/shard_map/ppermute | solution.py:303
  38.8 0.9 %collective-permute-start.13 = (f32[16,256]{1,0:T(8,128)S(1)}, f32[16,256]{1,0:T(8,128)S(1)}, u32[]{:S(2)}, u32[]{:S(2)}) collective-permute-start(f32[16,256]{1,0:T(8,128)S(1)} %get-tuple-element.76.refs_14_), channel_id=1, source_target_pairs={{0,3},{1,2},{2,1},{3,0},{4,7},{5,6},{6,5},{7,4},{8,11},{9,10},{10,... | collective-permute-start | bytes 49160 | tf_op jit(solution)/shard_map/ppermute | solution.py:303
  39.7 0.8 %collective-permute-start.9 = (f32[9,16,128]{2,1,0:T(8,128)S(1)}, f32[9,16,128]{2,1,0:T(8,128)S(1)}, u32[]{:S(2)}, u32[]{:S(2)}) collective-permute-start(f32[9,16,128]{2,1,0:T(8,128)S(1)} %get-tuple-element.72.refs_10_), channel_id=1, source_target_pairs={{0,16},{16,0},{1,17},{17,1},{2,18},{18,2},{3,19},{19,3},{4,20},{20... | collective-permute-start | bytes 221192 | tf_op jit(solution)/shard_map/ppermute | solution.py:303
  40.5 0.0 collective-permute-start.10
  40.5 1.6 %collective-permute-start.11 = (f32[9,16,128]{2,1,0:T(8,128)S(1)}, f32[9,16,128]{2,1,0:T(8,128)S(1)}, u32[]{:S(2)}, u32[]{:S(2)}) collective-permute-start(f32[9,16,128]{2,1,0:T(8,128)S(1)} %get-tuple-element.74.refs_12_), channel_id=1, source_target_pairs={{0,12},{4,8},{8,4},{12,0},{1,13},{5,9},{9,5},{13,1},{2,14},{6,10},... | collective-permute-start | bytes 221192 | tf_op jit(solution)/shard_map/ppermute | solution.py:303
  42.1 0.9 %shard_map.85.more_in = f32[3,8,8,128]{3,2,1,0:T(8,128)S(1)} custom-call(f32[8,256,128]{2,1,0:T(8,128)S(1)} %get-tuple-element.70.w_ref, f32[8,256,128]{2,1,0:T(8,128)S(1)} %get-tuple-element.68.source_ref.q_ref, f32[8,256,128]{2,1,0:T(8,128)S(1)} %get-tuple-element.51.source_ref.load_ref, f32[6,256,128]{2,1,0:T(8,128)S(1)} %get-tuple-element.71.weight_ref, ...), custom_call_target="tpu_custom_call" | custom-call | flops 8000000000 | bytes 1048576 | tf_op jit(solution)/shard_map/pallas_call | solution.py:35
  43.0 0.0 collective-permute-done.12.refs_18_
  43.0 1.3 %collective-permute-done.13.refs_19_ = f32[16,256]{1,0:T(8,128)S(1)} collective-permute-done((f32[16,256]{1,0:T(8,128)S(1)}, f32[16,256]{1,0:T(8,128)S(1)}, u32[]{:S(2)}, u32[]{:S(2)}) %collective-permute-start.13) | collective-permute-done | bytes 16416 | tf_op jit(solution)/shard_map/ppermute | solution.py:303
  44.4 0.0 collective-permute-done.9.refs_15_
  44.4 0.0 collective-permute-done.10.refs_16_
  44.4 0.0 collective-permute-done.11.refs_17_
  44.4 0.2 shard_map.86
  44.6 12.0 %all_to_all.16 = f32[32,1,128]{2,1,0:T(1,128)S(1)} all-to-all(f32[32,1,128]{2,1,0:T(1,128)S(1)} %bitcast.10), channel_id=1, replica_groups=mesh['span'=2,'height'=4,'depth'=4] {'span','height','depth'}, dimensions={0} | all-to-all | bytes 32768 | tf_op jit(solution)/shard_map/all_to_all | solution.py:318
  56.6 1.8 %shard_map.87 = (f32[256,128]{1,0:T(8,128)S(1)}, bf16[32,17,128]{2,1,0:T(8,128)(2,1)S(1)}, f32[8,256,128]{2,1,0:T(8,128)}) custom-call(s32[3]{0:T(128)S(4)} %get-tuple-element.48.coords_ref, f32[32,128]{1,0:T(8,128)S(1)} %bitcast.9, f32[256,128]{1,0:T(8,128)S(1)} %shard_map.78.refs_0_.ks_ref, f32[256,128]{1,0:T(8,128)S(1)} %get-tuple-element.56.phase_ref.refs_1_, ...), custom_call_target="tpu_custom_call" | custom-call | bytes 1048576 | tf_op jit(solution)/shard_map/pallas_call | solution.py:35
  58.4 11.0 %all_to_all.17.in_ref = bf16[32,17,128]{2,1,0:T(8,128)(2,1)S(1)} all-to-all(bf16[32,17,128]{2,1,0:T(8,128)(2,1)S(1)} %get-tuple-element.84), channel_id=1, replica_groups=mesh['span'=2,'height'=4,'depth'=4] {'span','height','depth'}, dimensions={0} | all-to-all | bytes 278528 | tf_op jit(solution)/shard_map/all_to_all | solution.py:318
  69.4 1.1 %shard_map.88 = (f32[256,128]{1,0:T(8,128)}, f32[256,128]{1,0:T(8,128)}) custom-call(s32[3]{0:T(128)S(4)} %get-tuple-element.48.coords_ref, bf16[32,17,128]{2,1,0:T(8,128)(2,1)S(1)} %all_to_all.17.in_ref, f32[256,128]{1,0:T(8,128)S(1)} %get-tuple-element.85.sens_ref, f32[256,128]{1,0:T(8,128)S(1)} %get-tuple-element.69.refs_0_.start_ref, ...), custom_call_target="tpu_custom_call" | custom-call | bytes 1048576 | tf_op jit(solution)/shard_map/pallas_call | solution.py:35
Async XLA Ops:
  3.3 6.1 %collective-permute-start = (bf16[8,8,512]{2,1,0:T(8,128)(2,1)S(1)}, bf16[8,8,512]{2,1,0:T(8,128)(2,1)S(1)}, u32[]{:S(2)}, u32[]{:S(2)}) collective-permute-start(bf16[8,8,512]{2,1,0:T(8,128)(2,1)S(1)} %get-tuple-element.50), channel_id=1, source_target_pairs={{0,16},{16,0},{1,17},{17,1},{2,18},{18,2},{3,19},{19,3},{4,20},{20... | collective-permute-start | bytes 196616 | tf_op jit(solution)/shard_map/ppermute | solution.py:311
  10.0 5.0 %collective-permute-start.1 = (f32[8,8,512]{2,1,0:T(8,128)S(1)}, f32[8,8,512]{2,1,0:T(8,128)S(1)}, u32[]{:S(2)}, u32[]{:S(2)}) collective-permute-start(f32[8,8,512]{2,1,0:T(8,128)S(1)} %shard_map.77), channel_id=1, source_target_pairs={{0,16},{16,0},{1,17},{17,1},{2,18},{18,2},{3,19},{19,3},{4,20},{20... | collective-permute-start | bytes 393224 | tf_op jit(solution)/shard_map/ppermute | solution.py:311
  16.1 8.3 %collective-permute-start.5 = (f32[16,256]{1,0:T(8,128)S(1)}, f32[16,256]{1,0:T(8,128)S(1)}, u32[]{:S(2)}, u32[]{:S(2)}) collective-permute-start(f32[16,256]{1,0:T(8,128)S(1)} %get-tuple-element.64.refs_3_), channel_id=1, source_target_pairs={{0,1},{1,0},{2,3},{3,2},{4,5},{5,4},{6,7},{7,6},{8,9},{9,8},{10,11... | collective-permute-start | bytes 49160 | tf_op jit(solution)/shard_map/ppermute | solution.py:303
  17.7 6.7 %collective-permute-start.6 = (f32[16,256]{1,0:T(8,128)S(1)}, f32[16,256]{1,0:T(8,128)S(1)}, u32[]{:S(2)}, u32[]{:S(2)}) collective-permute-start(f32[16,256]{1,0:T(8,128)S(1)} %get-tuple-element.65.refs_4_), channel_id=1, source_target_pairs={{0,3},{1,2},{2,1},{3,0},{4,7},{5,6},{6,5},{7,4},{8,11},{9,10},{10,... | collective-permute-start | bytes 49160 | tf_op jit(solution)/shard_map/ppermute | solution.py:303
  20.2 4.4 %collective-permute-start.2 = (f32[10,16,128]{2,1,0:T(8,128)S(1)}, f32[10,16,128]{2,1,0:T(8,128)S(1)}, u32[]{:S(2)}, u32[]{:S(2)}) collective-permute-start(f32[10,16,128]{2,1,0:T(8,128)S(1)} %get-tuple-element.61.refs_0_), channel_id=1, source_target_pairs={{0,16},{16,0},{1,17},{17,1},{2,18},{18,2},{3,19},{19,3},{4,20},{20... | collective-permute-start | bytes 245768 | tf_op jit(solution)/shard_map/ppermute | solution.py:303
  21.4 3.2 %collective-permute-start.3 = (f32[10,16,128]{2,1,0:T(8,128)S(1)}, f32[10,16,128]{2,1,0:T(8,128)S(1)}, u32[]{:S(2)}, u32[]{:S(2)}) collective-permute-start(f32[10,16,128]{2,1,0:T(8,128)S(1)} %get-tuple-element.62.refs_1_), channel_id=1, source_target_pairs={{0,4},{4,0},{8,12},{12,8},{1,5},{5,1},{9,13},{13,9},{2,6},{6,2},{1... | collective-permute-start | bytes 245768 | tf_op jit(solution)/shard_map/ppermute | solution.py:303
  21.4 4.1 %collective-permute-start.4 = (f32[10,16,128]{2,1,0:T(8,128)S(1)}, f32[10,16,128]{2,1,0:T(8,128)S(1)}, u32[]{:S(2)}, u32[]{:S(2)}) collective-permute-start(f32[10,16,128]{2,1,0:T(8,128)S(1)} %get-tuple-element.63.refs_2_), channel_id=1, source_target_pairs={{0,12},{4,8},{8,4},{12,0},{1,13},{5,9},{9,5},{13,1},{2,14},{6,10},... | collective-permute-start | bytes 245768 | tf_op jit(solution)/shard_map/ppermute | solution.py:303
  27.6 4.5 %collective-permute-start.7 = (bf16[8,8,512]{2,1,0:T(8,128)(2,1)S(1)}, bf16[8,8,512]{2,1,0:T(8,128)(2,1)S(1)}, u32[]{:S(2)}, u32[]{:S(2)}) collective-permute-start(bf16[8,8,512]{2,1,0:T(8,128)(2,1)S(1)} %get-tuple-element.67), channel_id=1, source_target_pairs={{0,16},{16,0},{1,17},{17,1},{2,18},{18,2},{3,19},{19,3},{4,20},{20... | collective-permute-start | bytes 196616 | tf_op jit(solution)/shard_map/ppermute | solution.py:311
  32.7 4.3 %collective-permute-start.8 = (bf16[8,8,512]{2,1,0:T(8,128)(2,1)S(1)}, bf16[8,8,512]{2,1,0:T(8,128)(2,1)S(1)}, u32[]{:S(2)}, u32[]{:S(2)}) collective-permute-start(bf16[8,8,512]{2,1,0:T(8,128)(2,1)S(1)} %shard_map.82), channel_id=1, source_target_pairs={{0,16},{16,0},{1,17},{17,1},{2,18},{18,2},{3,19},{19,3},{4,20},{20... | collective-permute-start | bytes 196616 | tf_op jit(solution)/shard_map/ppermute | solution.py:311
  38.1 5.0 %collective-permute-start.12 = (f32[16,256]{1,0:T(8,128)S(1)}, f32[16,256]{1,0:T(8,128)S(1)}, u32[]{:S(2)}, u32[]{:S(2)}) collective-permute-start(f32[16,256]{1,0:T(8,128)S(1)} %get-tuple-element.75.refs_13_), channel_id=1, source_target_pairs={{0,1},{1,0},{2,3},{3,2},{4,5},{5,4},{6,7},{7,6},{8,9},{9,8},{10,11... | collective-permute-start | bytes 49160 | tf_op jit(solution)/shard_map/ppermute | solution.py:303
  38.8 5.5 %collective-permute-start.13 = (f32[16,256]{1,0:T(8,128)S(1)}, f32[16,256]{1,0:T(8,128)S(1)}, u32[]{:S(2)}, u32[]{:S(2)}) collective-permute-start(f32[16,256]{1,0:T(8,128)S(1)} %get-tuple-element.76.refs_14_), channel_id=1, source_target_pairs={{0,3},{1,2},{2,1},{3,0},{4,7},{5,6},{6,5},{7,4},{8,11},{9,10},{10,... | collective-permute-start | bytes 49160 | tf_op jit(solution)/shard_map/ppermute | solution.py:303
  39.7 4.6 %collective-permute-start.9 = (f32[9,16,128]{2,1,0:T(8,128)S(1)}, f32[9,16,128]{2,1,0:T(8,128)S(1)}, u32[]{:S(2)}, u32[]{:S(2)}) collective-permute-start(f32[9,16,128]{2,1,0:T(8,128)S(1)} %get-tuple-element.72.refs_10_), channel_id=1, source_target_pairs={{0,16},{16,0},{1,17},{17,1},{2,18},{18,2},{3,19},{19,3},{4,20},{20... | collective-permute-start | bytes 221192 | tf_op jit(solution)/shard_map/ppermute | solution.py:303
  40.5 3.9 %collective-permute-start.10 = (f32[9,16,128]{2,1,0:T(8,128)S(1)}, f32[9,16,128]{2,1,0:T(8,128)S(1)}, u32[]{:S(2)}, u32[]{:S(2)}) collective-permute-start(f32[9,16,128]{2,1,0:T(8,128)S(1)} %get-tuple-element.73.refs_11_), channel_id=1, source_target_pairs={{0,4},{4,0},{8,12},{12,8},{1,5},{5,1},{9,13},{13,9},{2,6},{6,2},{1... | collective-permute-start | bytes 221192 | tf_op jit(solution)/shard_map/ppermute | solution.py:303
  40.5 3.9 %collective-permute-start.11 = (f32[9,16,128]{2,1,0:T(8,128)S(1)}, f32[9,16,128]{2,1,0:T(8,128)S(1)}, u32[]{:S(2)}, u32[]{:S(2)}) collective-permute-start(f32[9,16,128]{2,1,0:T(8,128)S(1)} %get-tuple-element.74.refs_12_), channel_id=1, source_target_pairs={{0,12},{4,8},{8,4},{12,0},{1,13},{5,9},{9,5},{13,1},{2,14},{6,10},... | collective-permute-start | bytes 221192 | tf_op jit(solution)/shard_map/ppermute | solution.py:303
where the time goes:
time: 70.8 us; the launch traced here: 70.6 us
  blocking collectives  23 us (32%)
  Pallas kernels  19.6 us (28%)
  starting transfers between devices  16.9 us (24%)
  waiting for transfers between devices  10.4 us (15%)
  between operations  0.73 us (1%)
    all_to_all x2, blocking collectives, everyone(): lax.all_to_all(partial, AXES, split_axis=0, concat_axis=0, tiled=True)  23 us
    pallas_call x13, Pallas kernels, call(): pl.pallas_call(kernel, in_specs=[spec for _, spec in ins], out_specs=[spe...  17 us
    ppermute x10, starting transfers between devices, exchange(): received[faces.index((d, b))] = lax.ppermute(part, AXES[d], swap)  11 us
    ppermute x4, waiting for transfers between devices, to_owners(): lax.ppermute(part, 'span', [(i, (i + sign * shift) % spans) for i in rang...  7.9 us
    ppermute x4, starting transfers between devices, to_owners(): lax.ppermute(part, 'span', [(i, (i + sign * shift) % spans) for i in rang...  5.89 us
    pallas_call x1, Pallas kernels, local(): pl.pallas_call(first_kernel, in_specs=[HB] * 5, out_specs=[SM, VM, VM, VM...  2.61 us
    ppermute x10, waiting for transfers between devices, exchange(): received[faces.index((d, b))] = lax.ppermute(part, AXES[d], swap)  2.46 us
  transfers between devices with their start and end apart: 14, of which 6 were waited for; matrix products, arithmetic and copies ran while one was open for 0% of the time, Pallas kernels for 12%

commit v1 on v0

--- a/solution.py
+++ b/solution.py
@@ -214,9 +214,9 @@
             if d == 0:
                 x = face_position(coords_ref, d, b, X)
                 for t in range(T):
-                    out[index, pl.ds(t * 8, 8), :] = read_tile(x, t)
+                    out[index, pl.ds(t * 8, 8), :] = read_tile(x, t).astype(out.dtype)
             elif d == 1:
-                out[index] = read_rows(face_position(coords_ref, d, b, Y))
+                out[index] = read_rows(face_position(coords_ref, d, b, Y)).astype(out.dtype)
 
     def depth_faces(fields, coords_ref, count, addends=2):
         rows_i = lax.broadcasted_iota(jnp.int32, (2 * count, lanes), 0)
@@ -292,8 +292,8 @@
     def face_shape(d, count):
         return ((count, Y, Z), (count, X, Z), (-(-count // 8) * 8, X * Y))[d]
 
-    def face_outs(count):
-        return [(face_shape(d, count), F32, VM) for d, _ in faces]
+    def face_outs(count, dtype):
+        return [(face_shape(d, count), dtype, VM) for d, _ in faces]
 
     def exchange(payload):
         received = [None] * len(faces)
@@ -471,16 +471,16 @@
             )
             for (d, b), out in zip(faces, outs):
                 if d == 2:
-                    out[...] = depth[b * count : (b + 1) * count]
+                    out[...] = depth[b * count : (b + 1) * count].astype(out.dtype)
 
         return kernel
 
-    def to_field(begun, image, extras):
+    def to_field(begun, image, extras, dtype):
         result = call(
             faces_kernel(len(extras)),
             [(table, SM), (coords, SM), (image, VM), (begun, VM)]
             + [(e, VM) for e in extras],
-            [(field_shape, F32, VM)] + face_outs(loads + len(extras)),
+            [(field_shape, F32, VM)] + face_outs(loads + len(extras), dtype),
             scratch=[pltpu.VMEM((remote, 2, loads, cells), F32)],
             aliases={3: 0},
         )
@@ -506,7 +506,7 @@
         stiffness_kernel, [(void, SM), (phase_f, VM)], [(plain_shape, F32, VM)],
         flops=2000000000,
     )
-    z_field, z_sent, z_halo = to_field(begun, far_image, [ks, phase_f])
+    z_field, z_sent, z_halo = to_field(begun, far_image, [ks, phase_f], F32)
 
     def joined(mine, other):
         both = jnp.logical_and(mine > 0.0, other > 0.0)
@@ -638,7 +638,9 @@
     )
 
     far_image = far_part(far, BF16)
-    w_field, w_sent, w_halo = to_field(near_part(q_field, False)[0], far_image, [start])
+    w_field, w_sent, w_halo = to_field(
+        near_part(q_field, False)[0], far_image, [start], BF16
+    )
 
     products = 5
 
@@ -684,24 +686,24 @@
             faces, z_mine, z_other, w_mine, w_other, gaps, starts
         ):
             if d < 2:
-                begin[...] = w_b[loads]
+                begin[...] = w_b[loads].astype(F32)
                 for at in row_pieces(d):
                     weight = face_weight(coords_ref, d, b, z_a, z_b, (loads, at))
                     solid = weight > 0.0
                     for l in range(loads):
-                        tile = w_a[l, at, :]
-                        between = tile - w_b[l, at, :]
+                        tile = w_a[l, at, :].astype(F32)
+                        between = tile - w_b[l, at, :].astype(F32)
                         more_ref[2, l] += weight * tile * between
                         gap[1, l, at, :] = jnp.where(solid, between, 0.0)
                         gap[0, l, at, :] = jnp.where(
                             solid, z_a[l, at, :] - z_b[l, at, :], 0.0
                         )
             else:
-                begin[...] = w_b[pl.ds(loads, 8), :]
+                begin[...] = w_b[...].astype(F32)[loads : loads + 8]
                 weight = face_weight(coords_ref, d, b, z_a, z_b, (pl.ds(loads, 1), slice(None)))
                 solid = weight > 0.0
-                tile = w_a[pl.ds(0, loads), :]
-                between = tile - w_b[pl.ds(0, loads), :]
+                tile = w_a[...].astype(F32)[:loads]
+                between = tile - w_b[...].astype(F32)[:loads]
                 product = weight * tile * between
                 gap[1] = jnp.where(solid, between, 0.0)
                 gap[0] = jnp.where(

time: 70.8 us -> 70.3 us (level)
  no operation moved by 1% of the time
where the time goes in v1:
time: 70.3 us; the launch traced here: 70.1 us
  blocking collectives  22.6 us (32%)
  Pallas kernels  19.6 us (28%)
  starting transfers between devices  16.9 us (24%)
  waiting for transfers between devices  10.3 us (15%)
  between operations  0.73 us (1%)
    all_to_all x2, blocking collectives, everyone(): lax.all_to_all(partial, AXES, split_axis=0, concat_axis=0, tiled=True)  22.6 us
    pallas_call x13, Pallas kernels, call(): pl.pallas_call(kernel, in_specs=[spec for _, spec in ins], out_specs=[spe...  17 us
    ppermute x10, starting transfers between devices, exchange(): received[faces.index((d, b))] = lax.ppermute(part, AXES[d], swap)  11 us
    ppermute x4, waiting for transfers between devices, to_owners(): lax.ppermute(part, 'span', [(i, (i + sign * shift) % spans) for i in rang...  7.9 us
    ppermute x4, starting transfers between devices, to_owners(): lax.ppermute(part, 'span', [(i, (i + sign * shift) % spans) for i in rang...  5.89 us
    pallas_call x1, Pallas kernels, local(): pl.pallas_call(first_kernel, in_specs=[HB] * 5, out_specs=[SM, VM, VM, VM...  2.61 us
    ppermute x10, waiting for transfers between devices, exchange(): received[faces.index((d, b))] = lax.ppermute(part, AXES[d], swap)  2.37 us
  transfers between devices with their start and end apart: 14, of which 6 were waited for; matrix products, arithmetic and copies ran while one was open for 0% of the time, Pallas kernels for 12%

profile of v1, /device:TPU:0, one launch (start us, length us, event | category | flops | bytes accessed | tf_op | source)
XLA Modules:
  0.0 70.1 jit_solution(7698597582457836301)
XLA Ops:
  0.6 2.6 %first.1 = (s32[17]{0:T(128)S(4)}, bf16[8,8,512]{2,1,0:T(8,128)(2,1)S(1)}, f32[8,256,128]{2,1,0:T(8,128)S(1)}, f32[256,128]{1,0:T(8,128)S(1)}, bf16[8,512,512]{2...) custom-call(s32[2,2,16]{2,1,0:T(2,128)} %void_hbm.1, s32[2,2,16]{2,1,0:T(2,128)} %owner_hbm.1, ...), custom_call_target="tpu_custom_call" | custom-call | tf_op jit(solution)/shard_map/first/pallas_call | solution.py:365
  3.3 3.1 %collective-permute-start = (bf16[8,8,512]{2,1,0:T(8,128)(2,1)S(1)}, bf16[8,8,512]{2,1,0:T(8,128)(2,1)S(1)}, u32[]{:S(2)}, u32[]{:S(2)}) collective-permute-start(bf16[8,8,512]{2,1,0:T(8,128)(2,1)S(1)} %get-tuple-element.50), channel_id=1, source_target_pairs={{0,16},{16,0},{1,17},{17,1},{2,18},{18,2},{3,19},{19,3},{4,20},{20... | collective-permute-start | bytes 196616 | tf_op jit(solution)/shard_map/ppermute | solution.py:311
  6.3 3.0 %shard_map.76 = (f32[8,256,128]{2,1,0:T(8,128)S(1)}, bf16[8,512,512]{2,1,0:T(8,128)(2,1)S(1)}) custom-call(s32[17]{0:T(128)S(4)} %get-tuple-element.49.table_ref, s32[3]{0:T(128)S(4)} %get-tuple-element.48.coords_ref, f32[8,256,128]{2,1,0:T(8,128)S(1)} %get-tuple-element.51.source_ref.load_ref, bf16[8,512,512]{2,1,0:T(8,128)(2,1)S(1)} %get-tuple-element.52.blocks_ref, ...), custom_call_target="tpu_custom_call" | custom-call | flops 8000000000 | bytes 1048576 | tf_op jit(solution)/shard_map/pallas_call | solution.py:35
  9.3 0.0 collective-permute-done.rows_ref
  9.3 0.6 shard_map.77
  10.0 1.3 %collective-permute-start.1 = (f32[8,8,512]{2,1,0:T(8,128)S(1)}, f32[8,8,512]{2,1,0:T(8,128)S(1)}, u32[]{:S(2)}, u32[]{:S(2)}) collective-permute-start(f32[8,8,512]{2,1,0:T(8,128)S(1)} %shard_map.77), channel_id=1, source_target_pairs={{0,16},{16,0},{1,17},{17,1},{2,18},{18,2},{3,19},{19,3},{4,20},{20... | collective-permute-start | bytes 393224 | tf_op jit(solution)/shard_map/ppermute | solution.py:311
  11.2 0.1 shard_map.78.refs_0_.ks_ref
  11.3 3.6 %collective-permute-done.1.image_ref = f32[8,8,512]{2,1,0:T(8,128)S(1)} collective-permute-done((f32[8,8,512]{2,1,0:T(8,128)S(1)}, f32[8,8,512]{2,1,0:T(8,128)S(1)}, u32[]{:S(2)}, u32[]{:S(2)}) %collective-permute-start.1) | collective-permute-done | bytes 131104 | tf_op jit(solution)/shard_map/ppermute | solution.py:311
  14.9 1.1 %shard_map.79 = (f32[8,256,128]{2,1,0:T(8,128)S(1)}, f32[10,16,128]{2,1,0:T(8,128)S(1)}, f32[10,16,128]{2,1,0:T(8,128)S(1)}, f32[10,16,128]{2,1,0:T(8,128)S(1)},...) custom-call(s32[17]{0:T(128)S(4)} %get-tuple-element.49.table_ref, ...), custom_call_target="tpu_custom_call", output_to_operand_aliasing={{0}: (3, {})} | custom-call | bytes 1048576 | tf_op jit(solution)/shard_map/pallas_call | solution.py:35
  16.1 1.6 %collective-permute-start.5 = (f32[16,256]{1,0:T(8,128)S(1)}, f32[16,256]{1,0:T(8,128)S(1)}, u32[]{:S(2)}, u32[]{:S(2)}) collective-permute-start(f32[16,256]{1,0:T(8,128)S(1)} %get-tuple-element.64.refs_3_), channel_id=1, source_target_pairs={{0,1},{1,0},{2,3},{3,2},{4,5},{5,4},{6,7},{7,6},{8,9},{9,8},{10,11... | collective-permute-start | bytes 49160 | tf_op jit(solution)/shard_map/ppermute | solution.py:303
  17.7 2.5 %collective-permute-start.6 = (f32[16,256]{1,0:T(8,128)S(1)}, f32[16,256]{1,0:T(8,128)S(1)}, u32[]{:S(2)}, u32[]{:S(2)}) collective-permute-start(f32[16,256]{1,0:T(8,128)S(1)} %get-tuple-element.65.refs_4_), channel_id=1, source_target_pairs={{0,3},{1,2},{2,1},{3,0},{4,7},{5,6},{6,5},{7,4},{8,11},{9,10},{10,... | collective-permute-start | bytes 49160 | tf_op jit(solution)/shard_map/ppermute | solution.py:303
  20.2 1.3 %collective-permute-start.2 = (f32[10,16,128]{2,1,0:T(8,128)S(1)}, f32[10,16,128]{2,1,0:T(8,128)S(1)}, u32[]{:S(2)}, u32[]{:S(2)}) collective-permute-start(f32[10,16,128]{2,1,0:T(8,128)S(1)} %get-tuple-element.61.refs_0_), channel_id=1, source_target_pairs={{0,16},{16,0},{1,17},{17,1},{2,18},{18,2},{3,19},{19,3},{4,20},{20... | collective-permute-start | bytes 245768 | tf_op jit(solution)/shard_map/ppermute | solution.py:303
  21.4 0.0 collective-permute-start.3
  21.4 1.6 %collective-permute-start.4 = (f32[10,16,128]{2,1,0:T(8,128)S(1)}, f32[10,16,128]{2,1,0:T(8,128)S(1)}, u32[]{:S(2)}, u32[]{:S(2)}) collective-permute-start(f32[10,16,128]{2,1,0:T(8,128)S(1)} %get-tuple-element.63.refs_2_), channel_id=1, source_target_pairs={{0,12},{4,8},{8,4},{12,0},{1,13},{5,9},{9,5},{13,1},{2,14},{6,10},... | collective-permute-start | bytes 245768 | tf_op jit(solution)/shard_map/ppermute | solution.py:303
  23.0 1.3 %shard_map.80 = (f32[8,256,128]{2,1,0:T(8,128)S(1)}, f32[6,256,128]{2,1,0:T(8,128)S(1)}, f32[256,128]{1,0:T(8,128)S(1)}, f32[2,8,8,128]{3,2,1,0:T(8,128)S(1)}) custom-call(f32[8,256,128]{2,1,0:T(8,128)S(1)} %get-tuple-element.57.z_ref, f32[8,256,128]{2,1,0:T(8,128)S(1)} %get-tuple-element.51.source_ref.load_ref, f32[256,128]{1,0:T(8,128)S(1)} %shard_map.78.refs_0_.ks_ref, ...), custom_call_target="tpu_custom_call" | custom-call | flops 8000000000 | bytes 1048576 | tf_op jit(solution)/shard_map/pallas_call | solution.py:35
  24.4 0.0 collective-permute-done.5.refs_8_
  24.4 0.0 collective-permute-done.6.refs_9_
  24.4 0.2 collective-permute-done.2.refs_5_
  24.6 0.0 collective-permute-done.3.refs_6_
  24.6 0.9 %collective-permute-done.4.refs_7_ = f32[10,16,128]{2,1,0:T(8,128)S(1)} collective-permute-done((f32[10,16,128]{2,1,0:T(8,128)S(1)}, f32[10,16,128]{2,1,0:T(8,128)S(1)}, u32[]{:S(2)}, u32[]{:S(2)}) %collective-permute-start.4) | collective-permute-done | bytes 81952 | tf_op jit(solution)/shard_map/ppermute | solution.py:303
  25.5 2.1 %shard_map.81 = (f32[8,256,128]{2,1,0:T(8,128)S(1)}, f32[256,128]{1,0:T(8,128)S(1)}, f32[2,8,8,128]{3,2,1,0:T(8,128)S(1)}, bf16[8,8,512]{2,1,0:T(8,128)(2,1)S(1)}) custom-call(s32[3]{0:T(128)S(4)} %get-tuple-element.48.coords_ref, s32[17]{0:T(128)S(4)} %get-tuple-element.49.table_ref, ...), custom_call_target="tpu_custom_call", output_to_operand_aliasing={{0}: (2, {}), {1}: (3, {}), {2}: (4, {})} | custom-call | bytes 1048576 | tf_op jit(solution)/shard_map/pallas_call | solution.py:35
  27.6 0.8 %collective-permute-start.7 = (bf16[8,8,512]{2,1,0:T(8,128)(2,1)S(1)}, bf16[8,8,512]{2,1,0:T(8,128)(2,1)S(1)}, u32[]{:S(2)}, u32[]{:S(2)}) collective-permute-start(bf16[8,8,512]{2,1,0:T(8,128)(2,1)S(1)} %get-tuple-element.67), channel_id=1, source_target_pairs={{0,16},{16,0},{1,17},{17,1},{2,18},{18,2},{3,19},{19,3},{4,20},{20... | collective-permute-start | bytes 196616 | tf_op jit(solution)/shard_map/ppermute | solution.py:311
  28.3 3.8 %collective-permute-done.7.rows_ref = bf16[8,8,512]{2,1,0:T(8,128)(2,1)S(1)} collective-permute-done((bf16[8,8,512]{2,1,0:T(8,128)(2,1)S(1)}, bf16[8,8,512]{2,1,0:T(8,128)(2,1)S(1)}, u32[]{:S(2)}, u32[]{:S(2)}) %collective-permute-start.7) | collective-permute-done | bytes 65568 | tf_op jit(solution)/shard_map/ppermute | solution.py:311
  32.1 0.6 shard_map.82
  32.7 0.8 %collective-permute-start.8 = (bf16[8,8,512]{2,1,0:T(8,128)(2,1)S(1)}, bf16[8,8,512]{2,1,0:T(8,128)(2,1)S(1)}, u32[]{:S(2)}, u32[]{:S(2)}) collective-permute-start(bf16[8,8,512]{2,1,0:T(8,128)(2,1)S(1)} %shard_map.82), channel_id=1, source_target_pairs={{0,16},{16,0},{1,17},{17,1},{2,18},{18,2},{3,19},{19,3},{4,20},{20... | collective-permute-start | bytes 196616 | tf_op jit(solution)/shard_map/ppermute | solution.py:311
  33.5 3.0 %shard_map.83.begun_ref = f32[8,256,128]{2,1,0:T(8,128)S(1)} custom-call(s32[17]{0:T(128)S(4)} %get-tuple-element.49.table_ref, s32[3]{0:T(128)S(4)} %get-tuple-element.48.coords_ref, f32[8,256,128]{2,1,0:T(8,128)S(1)} %get-tuple-element.68.source_ref.q_ref, bf16[8,512,512]{2,1,0:T(8,128)(2,1)S(1)} %get-tuple-element.52.blocks_ref), custom_call_target="tpu_custom_call" | custom-call | flops 8000000000 | bytes 1048576 | tf_op jit(solution)/shard_map/pallas_call | solution.py:35
  36.5 0.5 collective-permute-done.8.image_ref
  37.0 1.0 %shard_map.84 = (f32[8,256,128]{2,1,0:T(8,128)S(1)}, bf16[9,16,128]{2,1,0:T(8,128)(2,1)S(1)}, bf16[9,16,128]{2,1,0:T(8,128)(2,1)S(1)}, bf16[9,16,128]{2,1,0:T(8,...) custom-call(s32[17]{0:T(128)S(4)} %get-tuple-element.49.table_ref, ...), custom_call_target="tpu_custom_call", output_to_operand_aliasing={{0}: (3, {})} | custom-call | bytes 1048576 | tf_op jit(solution)/shard_map/pallas_call | solution.py:35
  38.1 0.8 %collective-permute-start.12 = (bf16[16,256]{1,0:T(8,128)(2,1)S(1)}, bf16[16,256]{1,0:T(8,128)(2,1)S(1)}, u32[]{:S(2)}, u32[]{:S(2)}) collective-permute-start(bf16[16,256]{1,0:T(8,128)(2,1)S(1)} %get-tuple-element.75.refs_13_), channel_id=1, source_target_pairs={{0,1},{1,0},{2,3},{3,2},{4,5},{5,4},{6,7},{7,6},{8,9},{9,8},{10,11... | collective-permute-start | bytes 24584 | tf_op jit(solution)/shard_map/ppermute | solution.py:303
  38.8 0.9 %collective-permute-start.13 = (bf16[16,256]{1,0:T(8,128)(2,1)S(1)}, bf16[16,256]{1,0:T(8,128)(2,1)S(1)}, u32[]{:S(2)}, u32[]{:S(2)}) collective-permute-start(bf16[16,256]{1,0:T(8,128)(2,1)S(1)} %get-tuple-element.76.refs_14_), channel_id=1, source_target_pairs={{0,3},{1,2},{2,1},{3,0},{4,7},{5,6},{6,5},{7,4},{8,11},{9,10},{10,... | collective-permute-start | bytes 24584 | tf_op jit(solution)/shard_map/ppermute | solution.py:303
  39.7 0.8 %collective-permute-start.9 = (bf16[9,16,128]{2,1,0:T(8,128)(2,1)S(1)}, bf16[9,16,128]{2,1,0:T(8,128)(2,1)S(1)}, u32[]{:S(2)}, u32[]{:S(2)}) collective-permute-start(bf16[9,16,128]{2,1,0:T(8,128)(2,1)S(1)} %get-tuple-element.72.refs_10_), channel_id=1, source_target_pairs={{0,16},{16,0},{1,17},{17,1},{2,18},{18,2},{3,19},{19,3},{4,20},{20... | collective-permute-start | bytes 110600 | tf_op jit(solution)/shard_map/ppermute | solution.py:303
  40.5 0.0 collective-permute-start.10
  40.5 1.6 %collective-permute-start.11 = (bf16[9,16,128]{2,1,0:T(8,128)(2,1)S(1)}, bf16[9,16,128]{2,1,0:T(8,128)(2,1)S(1)}, u32[]{:S(2)}, u32[]{:S(2)}) collective-permute-start(bf16[9,16,128]{2,1,0:T(8,128)(2,1)S(1)} %get-tuple-element.74.refs_12_), channel_id=1, source_target_pairs={{0,12},{4,8},{8,4},{12,0},{1,13},{5,9},{9,5},{13,1},{2,14},{6,10},... | collective-permute-start | bytes 110600 | tf_op jit(solution)/shard_map/ppermute | solution.py:303
  42.1 0.9 %shard_map.85.more_in = f32[3,8,8,128]{3,2,1,0:T(8,128)S(1)} custom-call(f32[8,256,128]{2,1,0:T(8,128)S(1)} %get-tuple-element.70.w_ref, f32[8,256,128]{2,1,0:T(8,128)S(1)} %get-tuple-element.68.source_ref.q_ref, f32[8,256,128]{2,1,0:T(8,128)S(1)} %get-tuple-element.51.source_ref.load_ref, f32[6,256,128]{2,1,0:T(8,128)S(1)} %get-tuple-element.71.weight_ref, ...), custom_call_target="tpu_custom_call" | custom-call | flops 8000000000 | bytes 1048576 | tf_op jit(solution)/shard_map/pallas_call | solution.py:35
  43.0 0.0 collective-permute-done.12.refs_18_
  43.0 1.2 %collective-permute-done.13.refs_19_ = bf16[16,256]{1,0:T(8,128)(2,1)S(1)} collective-permute-done((bf16[16,256]{1,0:T(8,128)(2,1)S(1)}, bf16[16,256]{1,0:T(8,128)(2,1)S(1)}, u32[]{:S(2)}, u32[]{:S(2)}) %collective-permute-start.13) | collective-permute-done | bytes 8224 | tf_op jit(solution)/shard_map/ppermute | solution.py:303
  44.3 0.0 collective-permute-done.9.refs_15_
  44.3 0.0 collective-permute-done.10.refs_16_
  44.3 0.0 collective-permute-done.11.refs_17_
  44.3 0.2 shard_map.86
  44.5 11.6 %all_to_all.16 = f32[32,1,128]{2,1,0:T(1,128)S(1)} all-to-all(f32[32,1,128]{2,1,0:T(1,128)S(1)} %bitcast.10), channel_id=1, replica_groups=mesh['span'=2,'height'=4,'depth'=4] {'span','height','depth'}, dimensions={0} | all-to-all | bytes 32768 | tf_op jit(solution)/shard_map/all_to_all | solution.py:318
  56.1 1.8 %shard_map.87 = (f32[256,128]{1,0:T(8,128)S(1)}, bf16[32,17,128]{2,1,0:T(8,128)(2,1)S(1)}, f32[8,256,128]{2,1,0:T(8,128)}) custom-call(s32[3]{0:T(128)S(4)} %get-tuple-element.48.coords_ref, f32[32,128]{1,0:T(8,128)S(1)} %bitcast.9, f32[256,128]{1,0:T(8,128)S(1)} %shard_map.78.refs_0_.ks_ref, f32[256,128]{1,0:T(8,128)S(1)} %get-tuple-element.56.phase_ref.refs_1_, ...), custom_call_target="tpu_custom_call" | custom-call | bytes 1048576 | tf_op jit(solution)/shard_map/pallas_call | solution.py:35
  57.9 11.0 %all_to_all.17.in_ref = bf16[32,17,128]{2,1,0:T(8,128)(2,1)S(1)} all-to-all(bf16[32,17,128]{2,1,0:T(8,128)(2,1)S(1)} %get-tuple-element.84), channel_id=1, replica_groups=mesh['span'=2,'height'=4,'depth'=4] {'span','height','depth'}, dimensions={0} | all-to-all | bytes 278528 | tf_op jit(solution)/shard_map/all_to_all | solution.py:318
  69.0 1.1 %shard_map.88 = (f32[256,128]{1,0:T(8,128)}, f32[256,128]{1,0:T(8,128)}) custom-call(s32[3]{0:T(128)S(4)} %get-tuple-element.48.coords_ref, bf16[32,17,128]{2,1,0:T(8,128)(2,1)S(1)} %all_to_all.17.in_ref, f32[256,128]{1,0:T(8,128)S(1)} %get-tuple-element.85.sens_ref, f32[256,128]{1,0:T(8,128)S(1)} %get-tuple-element.69.refs_0_.start_ref, ...), custom_call_target="tpu_custom_call" | custom-call | bytes 1048576 | tf_op jit(solution)/shard_map/pallas_call | solution.py:35
Async XLA Ops:
  3.3 6.1 %collective-permute-start = (bf16[8,8,512]{2,1,0:T(8,128)(2,1)S(1)}, bf16[8,8,512]{2,1,0:T(8,128)(2,1)S(1)}, u32[]{:S(2)}, u32[]{:S(2)}) collective-permute-start(bf16[8,8,512]{2,1,0:T(8,128)(2,1)S(1)} %get-tuple-element.50), channel_id=1, source_target_pairs={{0,16},{16,0},{1,17},{17,1},{2,18},{18,2},{3,19},{19,3},{4,20},{20... | collective-permute-start | bytes 196616 | tf_op jit(solution)/shard_map/ppermute | solution.py:311
  10.0 5.0 %collective-permute-start.1 = (f32[8,8,512]{2,1,0:T(8,128)S(1)}, f32[8,8,512]{2,1,0:T(8,128)S(1)}, u32[]{:S(2)}, u32[]{:S(2)}) collective-permute-start(f32[8,8,512]{2,1,0:T(8,128)S(1)} %shard_map.77), channel_id=1, source_target_pairs={{0,16},{16,0},{1,17},{17,1},{2,18},{18,2},{3,19},{19,3},{4,20},{20... | collective-permute-start | bytes 393224 | tf_op jit(solution)/shard_map/ppermute | solution.py:311
  16.1 8.3 %collective-permute-start.5 = (f32[16,256]{1,0:T(8,128)S(1)}, f32[16,256]{1,0:T(8,128)S(1)}, u32[]{:S(2)}, u32[]{:S(2)}) collective-permute-start(f32[16,256]{1,0:T(8,128)S(1)} %get-tuple-element.64.refs_3_), channel_id=1, source_target_pairs={{0,1},{1,0},{2,3},{3,2},{4,5},{5,4},{6,7},{7,6},{8,9},{9,8},{10,11... | collective-permute-start | bytes 49160 | tf_op jit(solution)/shard_map/ppermute | solution.py:303
  17.7 6.7 %collective-permute-start.6 = (f32[16,256]{1,0:T(8,128)S(1)}, f32[16,256]{1,0:T(8,128)S(1)}, u32[]{:S(2)}, u32[]{:S(2)}) collective-permute-start(f32[16,256]{1,0:T(8,128)S(1)} %get-tuple-element.65.refs_4_), channel_id=1, source_target_pairs={{0,3},{1,2},{2,1},{3,0},{4,7},{5,6},{6,5},{7,4},{8,11},{9,10},{10,... | collective-permute-start | bytes 49160 | tf_op jit(solution)/shard_map/ppermute | solution.py:303
  20.2 4.4 %collective-permute-start.2 = (f32[10,16,128]{2,1,0:T(8,128)S(1)}, f32[10,16,128]{2,1,0:T(8,128)S(1)}, u32[]{:S(2)}, u32[]{:S(2)}) collective-permute-start(f32[10,16,128]{2,1,0:T(8,128)S(1)} %get-tuple-element.61.refs_0_), channel_id=1, source_target_pairs={{0,16},{16,0},{1,17},{17,1},{2,18},{18,2},{3,19},{19,3},{4,20},{20... | collective-permute-start | bytes 245768 | tf_op jit(solution)/shard_map/ppermute | solution.py:303
  21.4 3.2 %collective-permute-start.3 = (f32[10,16,128]{2,1,0:T(8,128)S(1)}, f32[10,16,128]{2,1,0:T(8,128)S(1)}, u32[]{:S(2)}, u32[]{:S(2)}) collective-permute-start(f32[10,16,128]{2,1,0:T(8,128)S(1)} %get-tuple-element.62.refs_1_), channel_id=1, source_target_pairs={{0,4},{4,0},{8,12},{12,8},{1,5},{5,1},{9,13},{13,9},{2,6},{6,2},{1... | collective-permute-start | bytes 245768 | tf_op jit(solution)/shard_map/ppermute | solution.py:303
  21.4 4.1 %collective-permute-start.4 = (f32[10,16,128]{2,1,0:T(8,128)S(1)}, f32[10,16,128]{2,1,0:T(8,128)S(1)}, u32[]{:S(2)}, u32[]{:S(2)}) collective-permute-start(f32[10,16,128]{2,1,0:T(8,128)S(1)} %get-tuple-element.63.refs_2_), channel_id=1, source_target_pairs={{0,12},{4,8},{8,4},{12,0},{1,13},{5,9},{9,5},{13,1},{2,14},{6,10},... | collective-permute-start | bytes 245768 | tf_op jit(solution)/shard_map/ppermute | solution.py:303
  27.6 4.5 %collective-permute-start.7 = (bf16[8,8,512]{2,1,0:T(8,128)(2,1)S(1)}, bf16[8,8,512]{2,1,0:T(8,128)(2,1)S(1)}, u32[]{:S(2)}, u32[]{:S(2)}) collective-permute-start(bf16[8,8,512]{2,1,0:T(8,128)(2,1)S(1)} %get-tuple-element.67), channel_id=1, source_target_pairs={{0,16},{16,0},{1,17},{17,1},{2,18},{18,2},{3,19},{19,3},{4,20},{20... | collective-permute-start | bytes 196616 | tf_op jit(solution)/shard_map/ppermute | solution.py:311
  32.7 4.3 %collective-permute-start.8 = (bf16[8,8,512]{2,1,0:T(8,128)(2,1)S(1)}, bf16[8,8,512]{2,1,0:T(8,128)(2,1)S(1)}, u32[]{:S(2)}, u32[]{:S(2)}) collective-permute-start(bf16[8,8,512]{2,1,0:T(8,128)(2,1)S(1)} %shard_map.82), channel_id=1, source_target_pairs={{0,16},{16,0},{1,17},{17,1},{2,18},{18,2},{3,19},{19,3},{4,20},{20... | collective-permute-start | bytes 196616 | tf_op jit(solution)/shard_map/ppermute | solution.py:311
  38.1 5.0 %collective-permute-start.12 = (bf16[16,256]{1,0:T(8,128)(2,1)S(1)}, bf16[16,256]{1,0:T(8,128)(2,1)S(1)}, u32[]{:S(2)}, u32[]{:S(2)}) collective-permute-start(bf16[16,256]{1,0:T(8,128)(2,1)S(1)} %get-tuple-element.75.refs_13_), channel_id=1, source_target_pairs={{0,1},{1,0},{2,3},{3,2},{4,5},{5,4},{6,7},{7,6},{8,9},{9,8},{10,11... | collective-permute-start | bytes 24584 | tf_op jit(solution)/shard_map/ppermute | solution.py:303
  38.8 5.4 %collective-permute-start.13 = (bf16[16,256]{1,0:T(8,128)(2,1)S(1)}, bf16[16,256]{1,0:T(8,128)(2,1)S(1)}, u32[]{:S(2)}, u32[]{:S(2)}) collective-permute-start(bf16[16,256]{1,0:T(8,128)(2,1)S(1)} %get-tuple-element.76.refs_14_), channel_id=1, source_target_pairs={{0,3},{1,2},{2,1},{3,0},{4,7},{5,6},{6,5},{7,4},{8,11},{9,10},{10,... | collective-permute-start | bytes 24584 | tf_op jit(solution)/shard_map/ppermute | solution.py:303
  39.7 4.5 %collective-permute-start.9 = (bf16[9,16,128]{2,1,0:T(8,128)(2,1)S(1)}, bf16[9,16,128]{2,1,0:T(8,128)(2,1)S(1)}, u32[]{:S(2)}, u32[]{:S(2)}) collective-permute-start(bf16[9,16,128]{2,1,0:T(8,128)(2,1)S(1)} %get-tuple-element.72.refs_10_), channel_id=1, source_target_pairs={{0,16},{16,0},{1,17},{17,1},{2,18},{18,2},{3,19},{19,3},{4,20},{20... | collective-permute-start | bytes 110600 | tf_op jit(solution)/shard_map/ppermute | solution.py:303
  40.5 3.8 %collective-permute-start.10 = (bf16[9,16,128]{2,1,0:T(8,128)(2,1)S(1)}, bf16[9,16,128]{2,1,0:T(8,128)(2,1)S(1)}, u32[]{:S(2)}, u32[]{:S(2)}) collective-permute-start(bf16[9,16,128]{2,1,0:T(8,128)(2,1)S(1)} %get-tuple-element.73.refs_11_), channel_id=1, source_target_pairs={{0,4},{4,0},{8,12},{12,8},{1,5},{5,1},{9,13},{13,9},{2,6},{6,2},{1... | collective-permute-start | bytes 110600 | tf_op jit(solution)/shard_map/ppermute | solution.py:303
  40.5 3.8 %collective-permute-start.11 = (bf16[9,16,128]{2,1,0:T(8,128)(2,1)S(1)}, bf16[9,16,128]{2,1,0:T(8,128)(2,1)S(1)}, u32[]{:S(2)}, u32[]{:S(2)}) collective-permute-start(bf16[9,16,128]{2,1,0:T(8,128)(2,1)S(1)} %get-tuple-element.74.refs_12_), channel_id=1, source_target_pairs={{0,12},{4,8},{8,4},{12,0},{1,13},{5,9},{9,5},{13,1},{2,14},{6,10},... | collective-permute-start | bytes 110600 | tf_op jit(solution)/shard_map/ppermute | solution.py:303
